TPU v7x, 32 devices: a whole 2x2x4 slice. The times are simulated.
32 devices in a mesh: group: 2 (over x), tp: 4 (over z), dp: 4 (over y, core).
Axes of the slice: x: 2, y: 2, z: 4, core: 2. Of those that a mesh axis runs over, the one named last changes fastest.
Arguments:
- image_slots: bfloat16 [128, 8192], P(('group', 'tp'), 'dp'), may hold values from -6 to 6
- image_cot: bfloat16 [128, 8192], P(('group', 'tp'), 'dp'), may hold values from -6 to 6
- text_rows: bfloat16 [64, 8192], P(('group', 'tp'), 'dp'), may hold values from -6 to 6
- text_cot: bfloat16 [64, 8192], P(('group', 'tp'), 'dp'), may hold values from -6 to 6
- destination: int32 [64, 1], P(('group', 'tp')), may hold values from 0 to 1; in each aligned block of 8 rows (0 to 7, 8 to 15, ...) at most 8 rows name the same one
- text_count: int32 [8], P(('group', 'tp')), may hold values from 1 to 8, 48 in all
- w_gate: bfloat16 [8192, 14336], P('dp', 'tp'), may hold values from -0.0625 to 0.0625
- w_up: bfloat16 [8192, 14336], P('dp', 'tp'), may hold values from -0.0625 to 0.0625
- w_down: bfloat16 [14336, 8192], P('tp', 'dp'), may hold values from -0.046875 to 0.046875
Outputs:
- image_grad: bfloat16 [64, 8192], P(('group', 'tp'), 'dp')
- text_grad: bfloat16 [64, 8192], P(('group', 'tp'), 'dp')
Inputs may be any that keep to these rules, and one draw needn't show every extreme that they name: In the rows of one block of 8 rows no group is named more than 8 times, and some block names one group exactly 8 times; destination[i] decides which slot of image_slots and image_cot holds row i. Each block of 8 text rows has text_count live rows first; some block is full.
All inputs are finite; a program needn't handle non-finite values.
Results may differ from a plain program's by a relative error of at most 0.025.
Values may be sent and summed in bfloat16 or wider, within the bound.
No kernel may reach another device: no remote copies, remote signals or barrier semaphores. Data moves between devices by JAX's collectives and lax.ppermute only.
A program may use at most 128 MiB of HBM per device.

v0:
```python
import jax
import jax.numpy as jnp
from jax import lax
from jax.sharding import PartitionSpec as P


def language_grads(combined, w_gate, w_up, w_down):
    feat_dev = w_gate.shape[0]
    hidden_dev = w_gate.shape[1]
    piece = lax.all_gather(combined, "tp", axis=0, tiled=True)
    inputs_part = piece[:, :feat_dev]
    cot_part = piece[:, feat_dev:]
    gate = jnp.dot(inputs_part, w_gate, preferred_element_type=jnp.float32)
    up = jnp.dot(inputs_part, w_up, preferred_element_type=jnp.float32)
    back = lax.dot_general(
        cot_part, w_down, (((1,), (1,)), ((), ())), preferred_element_type=jnp.float32
    )
    partial_value = jnp.concatenate([gate, up, back], axis=1)
    sums = lax.psum_scatter(
        partial_value.astype(jnp.bfloat16), "dp", scatter_dimension=0, tiled=True
    ).astype(jnp.float32)
    gate = sums[:, :hidden_dev]
    up = sums[:, hidden_dev : 2 * hidden_dev]
    back = sums[:, 2 * hidden_dev :]
    sigmoid_gate = jax.nn.sigmoid(gate)
    dgate = (back * up * sigmoid_gate * (1.0 + gate * (1.0 - sigmoid_gate))).astype(jnp.bfloat16)
    dup = (back * gate * sigmoid_gate).astype(jnp.bfloat16)
    stacked = jnp.concatenate([dgate, dup], axis=1)
    piece = lax.all_gather(stacked, "dp", axis=0, tiled=True)
    total = lax.dot_general(
        piece[:, :hidden_dev], w_gate, (((1,), (1,)), ((), ())), preferred_element_type=jnp.float32
    )
    terms = total + lax.dot_general(
        piece[:, hidden_dev:], w_up, (((1,), (1,)), ((), ())), preferred_element_type=jnp.float32
    )
    return lax.psum_scatter(terms.astype(jnp.bfloat16), "tp", scatter_dimension=0, tiled=True)


def per_device(
    image_slots, image_cot, text_rows, text_cot, destination, text_count, w_gate, w_up, w_down
):
    groups = lax.axis_size("group")
    slot_dev = image_slots.shape[0]
    capacity = slot_dev // groups
    image_dev = destination.shape[0]
    text_dev = text_rows.shape[0]
    target = destination[:, 0]
    position = lax.broadcasted_iota(jnp.int32, (image_dev, image_dev), 0)
    other = lax.broadcasted_iota(jnp.int32, (image_dev, image_dev), 1)
    same = (target[:, None] == target[None, :]) & (other < position)
    rank = jnp.sum(same.astype(jnp.int32), axis=1)
    column = target * capacity + rank
    slot_index = lax.broadcasted_iota(jnp.int32, (image_dev, slot_dev), 1)
    select = (column[:, None] == slot_index).astype(jnp.bfloat16)
    text_both = jnp.concatenate([text_rows, text_cot], axis=1)
    both = jnp.concatenate([image_slots, image_cot], axis=1)
    arrived = lax.all_to_all(both, "group", split_axis=0, concat_axis=0, tiled=True)
    picked = jnp.dot(select, arrived, preferred_element_type=jnp.float32).astype(jnp.bfloat16)
    combined = jnp.concatenate([picked, text_both], axis=0)
    grads = language_grads(combined, w_gate, w_up, w_down)
    image_grad = grads[:image_dev]
    text_part = grads[image_dev:]
    live = lax.broadcasted_iota(jnp.int32, (text_dev, 1), 0) < text_count[0]
    text_grad = jnp.where(live, text_part, jnp.zeros_like(text_part))
    return (image_grad, text_grad)


def solution(mesh):
    placed = (
        P(("group", "tp"), "dp"),
        P(("group", "tp"), "dp"),
        P(("group", "tp"), "dp"),
        P(("group", "tp"), "dp"),
        P(("group", "tp"), None),
        P(("group", "tp")),
        P("dp", "tp"),
        P("dp", "tp"),
        P("tp", "dp"),
    )
    return jax.shard_map(
        per_device,
        mesh=mesh,
        in_specs=placed,
        out_specs=(P(("group", "tp"), "dp"), P(("group", "tp"), "dp")),
        check_vma=False,
    )
```

profile of v0, /device:TPU:0, one launch (start us, length us, event | category | flops | bytes accessed | tf_op | source)
XLA Modules:
  0.0 142.4 jit_solution(585150537257338750)
XLA Ops:
  7.2 1.5 %maximum_bitcast_fusion = bf16[2,8,4096]{2,1,0:T(8,128)(2,1)} fusion(bf16[16,2048]{1,0:T(8,128)(2,1)} %param.10, bf16[16,2048]{1,0:T(8,128)(2,1)} %param.9), kind=kLoop, calls=%fused_computation.20 | loop fusion | flops 262144 | bytes 262144 | tf_op jit(solution)/shard_map/all_to_all | solution.py:57
  8.7 4.2 %all-to-all-start = ((bf16[2,8,4096]{2,1,0:T(8,128)(2,1)}), bf16[2,8,4096]{2,1,0:T(8,128)(2,1)S(1)}, u32[]{:S(2)}, u32[]{:S(2)}) async-start(bf16[2,8,4096]{2,1,0:T(8,128)(2,1)} %maximum_bitcast_fusion), calls=%async_computation | async-start | bytes 262144 | tf_op jit(solution)/shard_map/all_to_all | solution.py:57
  12.9 0.9 convert_reduce_fusion
  13.8 0.7 fusion.13
  14.5 3.0 %all-to-all-done = bf16[2,8,4096]{2,1,0:T(8,128)(2,1)S(1)} async-done(((bf16[2,8,4096]{2,1,0:T(8,128)(2,1)}), bf16[2,8,4096]{2,1,0:T(8,128)(2,1)S(1)}, u32[]{:S(2)}, u32[]{:S(2)}) %all-to-all-start) | async-done | bytes 131104 | tf_op jit(solution)/shard_map/all_to_all | solution.py:57
  17.5 0.2 convolution_convert_fusion.3
  17.7 0.8 maximum_maximum_fusion
  18.5 15.6 %all_gather.6 = bf16[64,4096]{1,0:T(8,128)(2,1)S(1)} all-gather(bf16[16,4096]{1,0:T(8,128)(2,1)S(1)} %maximum_maximum_fusion), channel_id=1, replica_groups=mesh['group'=2,'tp'=4,'dp'=4] {'tp'}, dimensions={0}, use_global_device_ids=true | all-gather | bytes 655360 | tf_op jit(solution)/shard_map/all_gather | solution.py:10
  34.1 9.9 %convolution_convert_fusion = bf16[64,3584]{1,0:T(8,128)(2,1)S(1)} fusion(bf16[3584,2048]{1,0:T(8,128)(2,1)} %param.17, bf16[64,4096]{1,0:T(8,128)(2,1)S(1)} %all_gather.6), kind=kOutput, calls=%fused_computation | convolution fusion | flops 939753472 | bytes 15400960 | tf_op jit(solution)/shard_map/dot_general | solution.py:15
  43.9 0.0 slice-start.2
  44.0 8.0 %convolution_convert_fusion.1 = bf16[64,3584]{1,0:T(8,128)(2,1)S(1)} fusion(bf16[2048,3584]{1,0:T(8,128)(2,1)} %param.16, bf16[64,4096]{1,0:T(8,128)(2,1)S(1)} %all_gather.6), kind=kOutput, calls=%fused_computation.1 | convolution fusion | flops 939753472 | bytes 15400960 | tf_op jit(solution)/shard_map/dot_general | solution.py:14
  52.0 2.6 %convolution_convert_fusion.2 = bf16[64,3584]{1,0:T(8,128)(2,1)S(1)} fusion(bf16[2048,3584]{1,0:T(8,128)(2,1)S(1)} %bitcast.20, bf16[64,4096]{1,0:T(8,128)(2,1)S(1)} %all_gather.6), kind=kOutput, calls=%fused_computation.2 | convolution fusion | flops 939753472 | bytes 15400960 | tf_op jit(solution)/shard_map/dot_general | solution.py:13
  54.6 1.2 pad_maximum_fusion
  55.8 0.0 reduce-scatter.3.cloned.1.call-update
  55.8 0.0 reduce-scatter.5.cloned.1.call-start
  55.9 27.5 %reduce-scatter.3.cloned.1.call-done = bf16[16,10752]{1,0:T(8,128)(2,1)} async-done(((bf16[64,10752]{1,0:T(8,128)(2,1)}), bf16[16,10752]{1,0:T(8,128)(2,1)}) %reduce-scatter.3.cloned.1.call-update) | async-done | bytes 344080 | tf_op jit(solution)/shard_map/reduce_scatter | solution.py:19
  83.4 1.0 convert_element_type.22
  84.4 0.1 fusion.9
  84.6 8.7 %all_gather.7 = bf16[64,7168]{1,0:T(8,128)(2,1)S(1)} all-gather(bf16[16,7168]{1,0:T(8,128)(2,1)S(1)} %pad_maximum_fusion.1), channel_id=1, replica_groups=mesh['group'=2,'tp'=4,'dp'=4] {'dp'}, dimensions={0}, use_global_device_ids=true | all-gather | bytes 1146880 | tf_op jit(solution)/shard_map/all_gather | solution.py:29
  93.3 9.7 %fusion.2 = f32[64,2048]{1,0:T(8,128)S(1)} fusion(bf16[2048,3584]{1,0:T(8,128)(2,1)} %param.15, bf16[64,7168]{1,0:T(8,128)(2,1)S(1)} %all_gather.7), kind=kOutput, calls=%fused_computation.8 | convolution fusion | flops 939524096 | bytes 15663104 | tf_op jit(solution)/shard_map/dot_general | solution.py:30
  102.9 10.4 %fusion = bf16[64,2048]{1,0:T(8,128)(2,1)} fusion(f32[64,2048]{1,0:T(8,128)S(1)} %fusion.2, bf16[2048,3584]{1,0:T(8,128)(2,1)} %param.16, bf16[64,7168]{1,0:T(8,128)(2,1)S(1)} %all_gather.7), kind=kOutput, calls=%fused_computation.5 | convolution fusion | flops 939786240 | bytes 15925248 | tf_op jit(solution)/shard_map/dot_general | solution.py:33
  113.3 0.0 reduce-scatter.5.cloned.1.call-update
  114.0 20.1 %reduce-scatter.5.cloned.1.call-done = bf16[16,2048]{1,0:T(8,128)(2,1)} async-done(((bf16[64,2048]{1,0:T(8,128)(2,1)}), bf16[16,2048]{1,0:T(8,128)(2,1)}) %reduce-scatter.5.cloned.1.call-update) | async-done | bytes 65552 | tf_op jit(solution)/shard_map/reduce_scatter | solution.py:36
  134.1 1.5 %slice_select_fusion = (bf16[8,2048]{1,0:T(8,128)(2,1)}, bf16[8,2048]{1,0:T(8,128)(2,1)}) fusion(bf16[16,2048]{1,0:T(8,128)(2,1)} %reduce-scatter.5.cloned.1.call-done, pred[8]{0:T(512)(128)(4,1)S(1)} %iota_compare_fusion.3), kind=kLoop, calls=%fused_computation.23 | loop fusion | flops 16384 | bytes 131080 | tf_op jit(solution)/shard_map/jit(_where)/select_n | solution.py:64
  (11 shorter events, 0.0 us)
Async XLA Ops:
  8.7 8.8 %all-to-all-start = ((bf16[2,8,4096]{2,1,0:T(8,128)(2,1)}), bf16[2,8,4096]{2,1,0:T(8,128)(2,1)S(1)}, u32[]{:S(2)}, u32[]{:S(2)}) async-start(bf16[2,8,4096]{2,1,0:T(8,128)(2,1)} %maximum_bitcast_fusion), calls=%async_computation | async-start | bytes 262144 | tf_op jit(solution)/shard_map/all_to_all | solution.py:57
  12.9 70.5 %reduce-scatter.3.cloned.1.call-start = ((), (), s32[]{:S(2)}) async-start(), calls=%async_computation.3 | async-start | bytes 1720320 | tf_op jit(solution)/shard_map/reduce_scatter | solution.py:19
  34.1 17.8 %slice-start = ((s8[14680064]{0:T(1024)(128)(4,1)}), s8[4194304]{0:T(1024)(128)(4,1)S(1)}, s32[]{:S(2)}) async-start(s8[14680064]{0:T(1024)(128)(4,1)} %bitcast.19), calls=%async_computation.5 | async-start | bytes 8388608
  34.1 17.9 %slice-start.1 = ((s8[14680064]{0:T(1024)(128)(4,1)}), s8[2097152]{0:T(1024)(128)(4,1)S(1)}, s32[]{:S(2)}) async-start(s8[14680064]{0:T(1024)(128)(4,1)} %bitcast.19), calls=%async_computation.6 | async-start | bytes 4194304
  43.9 8.0 %slice-start.2 = ((s8[14680064]{0:T(1024)(128)(4,1)}), s8[4194304]{0:T(1024)(128)(4,1)S(1)}, s32[]{:S(2)}) async-start(s8[14680064]{0:T(1024)(128)(4,1)} %bitcast.19), calls=%async_computation.7 | async-start | bytes 8388608
  43.9 8.0 %slice-start.3 = ((s8[14680064]{0:T(1024)(128)(4,1)}), s8[4194304]{0:T(1024)(128)(4,1)S(1)}, s32[]{:S(2)}) async-start(s8[14680064]{0:T(1024)(128)(4,1)} %bitcast.19), calls=%async_computation.8 | async-start | bytes 8388608
  55.8 78.3 %reduce-scatter.5.cloned.1.call-start = ((), (), s32[]{:S(2)}) async-start(), calls=%async_computation.4 | async-start | bytes 327680 | tf_op jit(solution)/shard_map/reduce_scatter | solution.py:36
Sparse Core Ops, SparseCore 0:
  55.9 27.4 reduce-scatter.2
  113.5 20.5 reduce-scatter.4
where the time goes:
time: 143 us; the launch traced here: 142 us
  waiting for transfers between devices  50.6 us (35%)
  matrix products  40.7 us (28%)
  blocking collectives  24.3 us (17%)
  between operations  14.8 us (10%)
  other arithmetic  7.71 us (5%)
  starting transfers between devices  4.28 us (3%)
    reduce_scatter x1, waiting for transfers between devices, language_grads(): lax.psum_scatter(partial_value.astype(jnp.bfloat16), 'dp', scatter_dimens...  27.5 us
    reduce_scatter x1, waiting for transfers between devices, language_grads(): lax.psum_scatter(terms.astype(jnp.bfloat16), 'tp', scatter_dimension=0, t...  20.1 us
    all_gather x1, blocking collectives, language_grads(): piece = lax.all_gather(combined, 'tp', axis=0, tiled=True)  15.6 us
    dot_general x1, matrix products, language_grads(): lax.dot_general(piece[:, hidden_dev:], w_up, (((1,), (1,)), ((), ())), pr...  10.4 us
    dot_general x1, matrix products, language_grads(): lax.dot_general(cot_part, w_down, (((1,), (1,)), ((), ())), preferred_ele...  9.86 us
    dot_general x1, matrix products, language_grads(): lax.dot_general(piece[:, :hidden_dev], w_gate, (((1,), (1,)), ((), ())),...  9.67 us
    all_gather x1, blocking collectives, language_grads(): piece = lax.all_gather(stacked, 'dp', axis=0, tiled=True)  8.72 us
    dot_general x1, matrix products, language_grads(): up = jnp.dot(inputs_part, w_up, preferred_element_type=jnp.float32)  7.95 us
  transfers between devices with their start and end apart: 3, of which 3 were waited for; matrix products, arithmetic and copies ran while one was open for 1% of the time, Pallas kernels for 0%

commit v1 on v0

v1 whole, which is shorter than its diff:
```python
import jax
import jax.numpy as jnp
from jax import lax
from jax.sharding import PartitionSpec as P

F32 = jnp.float32
BF16 = jnp.bfloat16
DIRECT = 4


def shifted(value, axis, shift):
    size = lax.axis_size(axis)
    return lax.ppermute(value, axis, [(i, (i + shift) % size) for i in range(size)])


def swapped(value, axis, bit):
    size = lax.axis_size(axis)
    return lax.ppermute(value, axis, [(i, i ^ bit) for i in range(size)])


def bits_of(size):
    return [1 << i for i in range(size.bit_length() - 1)]


def by_xor(blocks, index):
    for bit in bits_of(len(blocks)):
        flip = (index & bit) != 0
        blocks = [jnp.where(flip, blocks[j ^ bit], blocks[j]) for j in range(len(blocks))]
    return blocks


def gather_rows(value, axis):
    size = lax.axis_size(axis)
    if size > DIRECT:
        full = lax.all_gather(value, axis, axis=0, tiled=True)
        return jnp.split(full, size, axis=0)
    return [value] + [shifted(value, axis, k) for k in range(1, size)]


def scatter_rows(blocks, axis):
    size = lax.axis_size(axis)
    if size > DIRECT:
        joined = jnp.concatenate([b.astype(BF16) for b in blocks], axis=0)
        return lax.psum_scatter(joined, axis, scatter_dimension=0, tiled=True).astype(F32)
    total = blocks[0]
    for k in range(1, size):
        total = total + shifted(blocks[k].astype(BF16), axis, -k).astype(F32)
    return total


def halve(blocks, axis):
    size = lax.axis_size(axis)
    for bit in bits_of(size):
        count = len(blocks)
        keep = blocks[0::2]
        give = blocks[1::2]
        sent = jnp.concatenate([b.astype(BF16) for b in give], axis=0)
        got = jnp.split(swapped(sent, axis, bit), count // 2, axis=0)
        blocks = [a.astype(F32) + b.astype(F32) for a, b in zip(keep, got)]
    return blocks[0]


def double(value, axis):
    size = lax.axis_size(axis)
    blocks = [value]
    for bit in reversed(bits_of(size)):
        sent = jnp.concatenate(blocks, axis=0)
        got = jnp.split(swapped(sent, axis, bit), len(blocks), axis=0)
        blocks = [b for pair in zip(blocks, got) for b in pair]
    return blocks


def to_blocks(rows, count):
    return jnp.split(rows, count, axis=0)


def language_grads(image, text, w_gate, w_up, w_down):
    parts = lax.axis_size("dp")
    index = lax.axis_index("dp")
    feat = w_gate.shape[0]
    text_all = gather_rows(text, "tp")
    image_all = gather_rows(image, "tp")
    image_dev = image.shape[0]
    tps = len(image_all)
    rows = jnp.concatenate([b for pair in zip(image_all, text_all) for b in pair], axis=0)
    rows = jnp.concatenate(by_xor(to_blocks(rows, parts), index), axis=0)
    inputs_part = rows[:, :feat]
    cot_part = rows[:, feat:]
    back = lax.dot_general(cot_part, w_down, (((1,), (1,)), ((), ())), preferred_element_type=F32)
    back = halve(to_blocks(back, parts), "dp")
    gate = jnp.dot(inputs_part, w_gate, preferred_element_type=F32)
    gate = halve(to_blocks(gate, parts), "dp")
    up = jnp.dot(inputs_part, w_up, preferred_element_type=F32)
    up = halve(to_blocks(up, parts), "dp")
    sigmoid_gate = jax.nn.sigmoid(gate)
    dgate = (back * up * sigmoid_gate * (1.0 + gate * (1.0 - sigmoid_gate))).astype(BF16)
    dup = (back * gate * sigmoid_gate).astype(BF16)
    hidden = dgate.shape[1]
    both = double(jnp.concatenate([dgate, dup], axis=1), "dp")
    both = jnp.concatenate(both, axis=0)
    terms = lax.dot_general(both[:, :hidden], w_gate, (((1,), (1,)), ((), ())), preferred_element_type=F32)
    terms = terms + lax.dot_general(both[:, hidden:], w_up, (((1,), (1,)), ((), ())), preferred_element_type=F32)
    terms = jnp.concatenate(by_xor(to_blocks(terms, parts), index), axis=0)
    return scatter_rows(to_blocks(terms, tps), "tp")


def exchanged(both, capacity):
    groups = lax.axis_size("group")
    if groups != 2:
        arrived = lax.all_to_all(both, "group", split_axis=0, concat_axis=0, tiled=True)
        return arrived, jnp.int32(0)
    mine = lax.axis_index("group")
    first = both[:capacity]
    second = both[capacity:]
    own = jnp.where(mine == 0, first, second)
    give = jnp.where(mine == 0, second, first)
    return jnp.concatenate([own, swapped(give, "group", 1)], axis=0), mine


def per_device(
    image_slots, image_cot, text_rows, text_cot, destination, text_count, w_gate, w_up, w_down
):
    groups = lax.axis_size("group")
    slot_dev = image_slots.shape[0]
    capacity = slot_dev // groups
    image_dev = destination.shape[0]
    text_dev = text_rows.shape[0]
    text_both = jnp.concatenate([text_rows, text_cot], axis=1)
    both = jnp.concatenate([image_slots, image_cot], axis=1)
    arrived, first = exchanged(both, capacity)
    target = destination[:, 0]
    position = lax.broadcasted_iota(jnp.int32, (image_dev, image_dev), 0)
    other = lax.broadcasted_iota(jnp.int32, (image_dev, image_dev), 1)
    same = (target[:, None] == target[None, :]) & (other < position)
    rank = jnp.sum(same.astype(jnp.int32), axis=1)
    column = jnp.bitwise_xor(target, first) * capacity + rank
    slot_index = lax.broadcasted_iota(jnp.int32, (image_dev, slot_dev), 1)
    select = (column[:, None] == slot_index).astype(BF16)
    picked = jnp.dot(select, arrived, preferred_element_type=F32).astype(BF16)
    grads = language_grads(picked, text_both, w_gate, w_up, w_down)
    image_grad = grads[:image_dev].astype(BF16)
    text_part = grads[image_dev:].astype(BF16)
    live = lax.broadcasted_iota(jnp.int32, (text_dev, 1), 0) < text_count[0]
    text_grad = jnp.where(live, text_part, jnp.zeros_like(text_part))
    return (image_grad, text_grad)


def solution(mesh):
    placed = (
        P(("group", "tp"), "dp"),
        P(("group", "tp"), "dp"),
        P(("group", "tp"), "dp"),
        P(("group", "tp"), "dp"),
        P(("group", "tp"), None),
        P(("group", "tp")),
        P("dp", "tp"),
        P("dp", "tp"),
        P("tp", "dp"),
    )
    return jax.shard_map(
        per_device,
        mesh=mesh,
        in_specs=placed,
        out_specs=(P(("group", "tp"), "dp"), P(("group", "tp"), "dp")),
        check_vma=False,
    )
```

time: 143 us -> 100 us (0.70)
  waiting for transfers between devices: 50.6 us -> 24.9 us
  blocking collectives: 24.3 us -> 0 us
  starting transfers between devices: 4.28 us -> 22.3 us
  between operations: 14.8 us -> 1.52 us
  other arithmetic: 7.71 us -> 2.97 us
  matrix products: 40.7 us -> 44.9 us
  local copies, waits for them, and re-layouts: 0.02 us -> 3.33 us
    reduce_scatter x2 -> x0, waiting for transfers between devices: 47.6 us -> none  [the longest x1 27.5 us: language_grads(): lax.psum_scatter(partial_value.astype(jnp.bfloat16), 'dp', scatter_dimens...]
    ppermute x0 -> x18, waiting for transfers between devices: none -> 24.9 us  [the longest x9 13.5 us: swapped(): return lax.ppermute(value, axis, [(i, i ^ bit) for i in range(size)])]
    all_gather x2 -> x0, blocking collectives: 24.3 us -> none  [the longest x1 15.6 us: language_grads(): piece = lax.all_gather(combined, 'tp', axis=0, tiled=True)]
    ppermute x0 -> x18, starting transfers between devices: none -> 22.3 us  [the longest x9 13.2 us: shifted(): lax.ppermute(value, axis, [(i, (i + shift) % size) for i in range(size)])]
    dot_general x5, matrix products: 30.8 us -> 35.2 us  [the longest x1 9.68 us: language_grads(): lax.dot_general(both[:, :hidden], w_gate, (((1,), (1,)), ((), ())), prefe...]
    all_to_all x1 -> x0, starting transfers between devices: 4.23 us -> none  [per_device(): lax.all_to_all(both, 'group', split_axis=0, concat_axis=0, tiled=True)]
    all_to_all x1 -> x0, waiting for transfers between devices: 2.98 us -> none  [per_device(): lax.all_to_all(both, 'group', split_axis=0, concat_axis=0, tiled=True)]
    concatenate x3 -> x7, other arithmetic: 2.01 us -> 0.2 us  [the longest x1 0.06 us: language_grads(): both = jnp.concatenate(both, axis=0)]
  transfers between devices with their start and end apart: 3 -> 18, of which waited for: 3 -> 8; matrix products, arithmetic and copies ran while one was open for 1% -> 21% of each run, Pallas kernels for 0% -> 0%
where the time goes in v1:
time: 100 us; the launch traced here: 99.9 us
  matrix products  44.9 us (45%)
  waiting for transfers between devices  24.9 us (25%)
  starting transfers between devices  22.3 us (22%)
  local copies, waits for them, and re-layouts  3.33 us (3%)
  other arithmetic  2.97 us (3%)
  between operations  1.52 us (2%)
    ppermute x9, waiting for transfers between devices, swapped(): return lax.ppermute(value, axis, [(i, i ^ bit) for i in range(size)])  13.5 us
    ppermute x9, starting transfers between devices, shifted(): lax.ppermute(value, axis, [(i, (i + shift) % size) for i in range(size)])  13.2 us
    ppermute x9, waiting for transfers between devices, shifted(): lax.ppermute(value, axis, [(i, (i + shift) % size) for i in range(size)])  11.4 us
    dot_general x1, matrix products, language_grads(): lax.dot_general(cot_part, w_down, (((1,), (1,)), ((), ())), preferred_ele...  9.72 us
    dot_general x1, matrix products, language_grads(): lax.dot_general(both[:, :hidden], w_gate, (((1,), (1,)), ((), ())), prefe...  9.68 us
    dot_general x1, matrix products, language_grads(): lax.dot_general(both[:, hidden:], w_up, (((1,), (1,)), ((), ())), preferr...  9.67 us
    ppermute x9, starting transfers between devices, swapped(): return lax.ppermute(value, axis, [(i, i ^ bit) for i in range(size)])  9.13 us
    dot_general x1, matrix products, language_grads(): gate = jnp.dot(inputs_part, w_gate, preferred_element_type=F32)  7.8 us
  transfers between devices with their start and end apart: 18, of which 8 were waited for; matrix products, arithmetic and copies ran while one was open for 21% of the time, Pallas kernels for 0%

profile of v1, /device:TPU:0, one launch (start us, length us, event | category | flops | bytes accessed | tf_op | source)
XLA Modules:
  0.0 99.9 jit_solution(11713350730965478845)
XLA Ops:
  0.6 0.8 constant_dynamic-update-slice_fusion.1
  1.5 0.8 constant_dynamic-update-slice_fusion
  2.3 3.0 %collective-permute-start = (bf16[8,4096]{1,0:T(8,128)(2,1)S(1)}, bf16[8,4096]{1,0:T(8,128)(2,1)S(1)}, u32[]{:S(2)}, u32[]{:S(2)}) collective-permute-start(bf16[8,4096]{1,0:T(8,128)(2,1)S(1)} %get-tuple-element.20), channel_id=1, source_target_pairs={{0,16},{16,0},{1,17},{17,1},{2,18},{18,2},{3,19},{19,3},{4,20},{20... | collective-permute-start | bytes 196616 | tf_op jit(solution)/shard_map/ppermute | solution.py:18
  5.4 0.9 convert_reduce_fusion
  7.9 4.1 %collective-permute-start.1 = (bf16[8,4096]{1,0:T(8,128)(2,1)S(1)}, bf16[8,4096]{1,0:T(8,128)(2,1)S(1)}, u32[]{:S(2)}, u32[]{:S(2)}) collective-permute-start(bf16[8,4096]{1,0:T(8,128)(2,1)S(1)} %convolution_convert_fusion), channel_id=1, source_target_pairs={{0,12},{4,0},{8,4},{12,8},{1,13},{5,1},{9,5},{13,9},{2,14},{6,2},{... | collective-permute-start | bytes 196616 | tf_op jit(solution)/shard_map/ppermute | solution.py:13
  13.2 1.6 %collective-permute-start.6 = (bf16[8,4096]{1,0:T(8,128)(2,1)S(1)}, bf16[8,4096]{1,0:T(8,128)(2,1)S(1)}, u32[]{:S(2)}, u32[]{:S(2)}) collective-permute-start(bf16[8,4096]{1,0:T(8,128)(2,1)S(1)} %constant_dynamic-update-slice_fusion.2), channel_id=1, source_target_pairs={{0,4},{4,8},{8,12},{12,0},{1,5},{5,9},{9,13},{13,1},{2,6},{6,10},{... | collective-permute-start | bytes 196616 | tf_op jit(solution)/shard_map/ppermute | solution.py:13
  14.8 2.9 %collective-permute-start.3 = (bf16[8,4096]{1,0:T(8,128)(2,1)S(1)}, bf16[8,4096]{1,0:T(8,128)(2,1)S(1)}, u32[]{:S(2)}, u32[]{:S(2)}) collective-permute-start(bf16[8,4096]{1,0:T(8,128)(2,1)S(1)} %convolution_convert_fusion), channel_id=1, source_target_pairs={{0,8},{4,12},{8,0},{12,4},{1,9},{5,13},{9,1},{13,5},{2,10},{6,14},... | collective-permute-start | bytes 196616 | tf_op jit(solution)/shard_map/ppermute | solution.py:13
  17.7 6.3 %collective-permute-done.3 = bf16[8,4096]{1,0:T(8,128)(2,1)S(1)} collective-permute-done((bf16[8,4096]{1,0:T(8,128)(2,1)S(1)}, bf16[8,4096]{1,0:T(8,128)(2,1)S(1)}, u32[]{:S(2)}, u32[]{:S(2)}) %collective-permute-start.3) | collective-permute-done | bytes 65568 | tf_op jit(solution)/shard_map/ppermute | solution.py:13
  24.3 7.8 %fusion.32 = (bf16[64,3584]{1,0:T(8,128)(2,1)S(1)}, f32[64,3584]{1,0:T(8,128)S(1)}) fusion(bf16[2048,3584]{1,0:T(8,128)(2,1)} %param.15, bf16[64,4096]{1,0:T(8,128)(2,1)S(1)} %pad_maximum_fusion.1), kind=kOutput, calls=%fused_computation.84 | convolution fusion | flops 939753472 | bytes 16318464 | tf_op jit(solution)/shard_map/dot_general | solution.py:91
  32.2 9.7 %fusion.31 = (bf16[64,3584]{1,0:T(8,128)(2,1)S(1)}, f32[64,3584]{1,0:T(8,128)S(1)}) fusion(bf16[3584,2048]{1,0:T(8,128)(2,1)} %param.17, bf16[64,4096]{1,0:T(8,128)(2,1)S(1)} %pad_maximum_fusion.1), kind=kOutput, calls=%fused_computation.83 | convolution fusion | flops 939753472 | bytes 16318464 | tf_op jit(solution)/shard_map/dot_general | solution.py:89
  42.5 7.8 %fusion.30 = (bf16[64,3584]{1,0:T(8,128)(2,1)S(1)}, f32[64,3584]{1,0:T(8,128)S(1)}) fusion(bf16[2048,3584]{1,0:T(8,128)(2,1)} %param.16, bf16[64,4096]{1,0:T(8,128)(2,1)S(1)} %pad_maximum_fusion.1), kind=kOutput, calls=%fused_computation.82 | convolution fusion | flops 939753472 | bytes 16318464 | tf_op jit(solution)/shard_map/dot_general | solution.py:93
  50.5 1.6 %collective-permute-start.12 = (bf16[16,3584]{1,0:T(8,128)(2,1)S(1)}, bf16[16,3584]{1,0:T(8,128)(2,1)S(1)}, u32[]{:S(2)}, u32[]{:S(2)}) collective-permute-start(bf16[16,3584]{1,0:T(8,128)(2,1)S(1)} %fusion.9), channel_id=1, source_target_pairs={{0,2},{1,3},{2,0},{3,1},{4,6},{5,7},{6,4},{7,5},{8,10},{9,11},{10,... | collective-permute-start | bytes 344072 | tf_op jit(solution)/shard_map/ppermute | solution.py:18
  52.7 1.6 %collective-permute-start.10 = (bf16[16,3584]{1,0:T(8,128)(2,1)S(1)}, bf16[16,3584]{1,0:T(8,128)(2,1)S(1)}, u32[]{:S(2)}, u32[]{:S(2)}) collective-permute-start(bf16[16,3584]{1,0:T(8,128)(2,1)S(1)} %fusion.11), channel_id=1, source_target_pairs={{0,2},{1,3},{2,0},{3,1},{4,6},{5,7},{6,4},{7,5},{8,10},{9,11},{10,... | collective-permute-start | bytes 344072 | tf_op jit(solution)/shard_map/ppermute | solution.py:18
  54.3 2.3 %collective-permute-done.12 = bf16[16,3584]{1,0:T(8,128)(2,1)S(1)} collective-permute-done((bf16[16,3584]{1,0:T(8,128)(2,1)S(1)}, bf16[16,3584]{1,0:T(8,128)(2,1)S(1)}, u32[]{:S(2)}, u32[]{:S(2)}) %collective-permute-start.12) | collective-permute-done | bytes 114720 | tf_op jit(solution)/shard_map/ppermute | solution.py:18
  56.6 2.5 %collective-permute-done.8 = bf16[16,3584]{1,0:T(8,128)(2,1)S(1)} collective-permute-done((bf16[16,3584]{1,0:T(8,128)(2,1)S(1)}, bf16[16,3584]{1,0:T(8,128)(2,1)S(1)}, u32[]{:S(2)}, u32[]{:S(2)}) %collective-permute-start.8) | collective-permute-done | bytes 114720 | tf_op jit(solution)/shard_map/ppermute | solution.py:18
  59.1 2.0 %collective-permute-done.10 = bf16[16,3584]{1,0:T(8,128)(2,1)S(1)} collective-permute-done((bf16[16,3584]{1,0:T(8,128)(2,1)S(1)}, bf16[16,3584]{1,0:T(8,128)(2,1)S(1)}, u32[]{:S(2)}, u32[]{:S(2)}) %collective-permute-start.10) | collective-permute-done | bytes 114720 | tf_op jit(solution)/shard_map/ppermute | solution.py:18
  61.3 1.6 %collective-permute-start.13 = (bf16[16,7168]{1,0:T(8,128)(2,1)S(1)}, bf16[16,7168]{1,0:T(8,128)(2,1)S(1)}, u32[]{:S(2)}, u32[]{:S(2)}) collective-permute-start(bf16[16,7168]{1,0:T(8,128)(2,1)S(1)} %pad_maximum_fusion.6), channel_id=1, source_target_pairs={{0,2},{1,3},{2,0},{3,1},{4,6},{5,7},{6,4},{7,5},{8,10},{9,11},{10,... | collective-permute-start | bytes 688136 | tf_op jit(solution)/shard_map/ppermute | solution.py:18
  62.8 5.6 %collective-permute-done.13 = bf16[16,7168]{1,0:T(8,128)(2,1)S(1)} collective-permute-done((bf16[16,7168]{1,0:T(8,128)(2,1)S(1)}, bf16[16,7168]{1,0:T(8,128)(2,1)S(1)}, u32[]{:S(2)}, u32[]{:S(2)}) %collective-permute-start.13) | collective-permute-done | bytes 229408 | tf_op jit(solution)/shard_map/ppermute | solution.py:18
  69.2 1.2 %collective-permute-done.14 = bf16[32,7168]{1,0:T(8,128)(2,1)S(1)} collective-permute-done((bf16[32,7168]{1,0:T(8,128)(2,1)S(1)}, bf16[32,7168]{1,0:T(8,128)(2,1)S(1)}, u32[]{:S(2)}, u32[]{:S(2)}) %collective-permute-start.14) | collective-permute-done | bytes 458784 | tf_op jit(solution)/shard_map/ppermute | solution.py:18
  70.5 9.7 %fusion = f32[64,2048]{1,0:T(8,128)S(1)} fusion(bf16[2048,3584]{1,0:T(8,128)(2,1)} %param.16, bf16[64,7168]{1,0:T(8,128)(2,1)S(1)} %pad_maximum_fusion), kind=kOutput, calls=%fused_computation.4 | convolution fusion | flops 939524096 | bytes 15663104 | tf_op jit(solution)/shard_map/dot_general | solution.py:102
  80.2 9.7 %convolution_add_fusion = f32[64,2048]{1,0:T(8,128)S(1)} fusion(f32[64,2048]{1,0:T(8,128)S(1)} %fusion, bf16[2048,3584]{1,0:T(8,128)(2,1)} %param.15, bf16[64,7168]{1,0:T(8,128)(2,1)S(1)} %pad_maximum_fusion), kind=kOutput, calls=%fused_computation.1 | convolution fusion | flops 939655168 | bytes 16187392 | tf_op jit(solution)/shard_map/dot_general | solution.py:101
  89.9 1.9 %collective-permute-start.15 = (bf16[16,2048]{1,0:T(8,128)(2,1)S(1)}, bf16[16,2048]{1,0:T(8,128)(2,1)S(1)}, u32[]{:S(2)}, u32[]{:S(2)}) collective-permute-start(bf16[16,2048]{1,0:T(8,128)(2,1)S(1)} %get-tuple-element.4), channel_id=1, source_target_pairs={{0,12},{4,0},{8,4},{12,8},{1,13},{5,1},{9,5},{13,9},{2,14},{6,2},{... | collective-permute-start | bytes 196616 | tf_op jit(solution)/shard_map/ppermute | solution.py:13
  92.1 1.9 %collective-permute-start.17 = (bf16[16,2048]{1,0:T(8,128)(2,1)S(1)}, bf16[16,2048]{1,0:T(8,128)(2,1)S(1)}, u32[]{:S(2)}, u32[]{:S(2)}) collective-permute-start(bf16[16,2048]{1,0:T(8,128)(2,1)S(1)} %get-tuple-element.6), channel_id=1, source_target_pairs={{0,4},{4,8},{8,12},{12,0},{1,5},{5,9},{9,13},{13,1},{2,6},{6,10},{... | collective-permute-start | bytes 196616 | tf_op jit(solution)/shard_map/ppermute | solution.py:13
  94.2 4.9 %collective-permute-done.16 = bf16[16,2048]{1,0:T(8,128)(2,1)S(1)} collective-permute-done((bf16[16,2048]{1,0:T(8,128)(2,1)S(1)}, bf16[16,2048]{1,0:T(8,128)(2,1)S(1)}, u32[]{:S(2)}, u32[]{:S(2)}) %collective-permute-start.16) | collective-permute-done | bytes 65568 | tf_op jit(solution)/shard_map/ppermute | solution.py:13
  (51 shorter events, 6.3 us)
Async XLA Ops:
  2.3 5.4 %collective-permute-start = (bf16[8,4096]{1,0:T(8,128)(2,1)S(1)}, bf16[8,4096]{1,0:T(8,128)(2,1)S(1)}, u32[]{:S(2)}, u32[]{:S(2)}) collective-permute-start(bf16[8,4096]{1,0:T(8,128)(2,1)S(1)} %get-tuple-element.20), channel_id=1, source_target_pairs={{0,16},{16,0},{1,17},{17,1},{2,18},{18,2},{3,19},{19,3},{4,20},{20... | collective-permute-start | bytes 196616 | tf_op jit(solution)/shard_map/ppermute | solution.py:18
  7.9 9.8 %collective-permute-start.1 = (bf16[8,4096]{1,0:T(8,128)(2,1)S(1)}, bf16[8,4096]{1,0:T(8,128)(2,1)S(1)}, u32[]{:S(2)}, u32[]{:S(2)}) collective-permute-start(bf16[8,4096]{1,0:T(8,128)(2,1)S(1)} %convolution_convert_fusion), channel_id=1, source_target_pairs={{0,12},{4,0},{8,4},{12,8},{1,13},{5,1},{9,5},{13,9},{2,14},{6,2},{... | collective-permute-start | bytes 196616 | tf_op jit(solution)/shard_map/ppermute | solution.py:13
  12.8 11.3 %collective-permute-start.2 = (bf16[8,4096]{1,0:T(8,128)(2,1)S(1)}, bf16[8,4096]{1,0:T(8,128)(2,1)S(1)}, u32[]{:S(2)}, u32[]{:S(2)}) collective-permute-start(bf16[8,4096]{1,0:T(8,128)(2,1)S(1)} %constant_dynamic-update-slice_fusion.2), channel_id=1, source_target_pairs={{0,12},{4,0},{8,4},{12,8},{1,13},{5,1},{9,5},{13,9},{2,14},{6,2},{... | collective-permute-start | bytes 196616 | tf_op jit(solution)/shard_map/ppermute | solution.py:13
  13.2 10.8 %collective-permute-start.4 = (bf16[8,4096]{1,0:T(8,128)(2,1)S(1)}, bf16[8,4096]{1,0:T(8,128)(2,1)S(1)}, u32[]{:S(2)}, u32[]{:S(2)}) collective-permute-start(bf16[8,4096]{1,0:T(8,128)(2,1)S(1)} %constant_dynamic-update-slice_fusion.2), channel_id=1, source_target_pairs={{0,8},{4,12},{8,0},{12,4},{1,9},{5,13},{9,1},{13,5},{2,10},{6,14},... | collective-permute-start | bytes 196616 | tf_op jit(solution)/shard_map/ppermute | solution.py:13
  13.2 10.9 %collective-permute-start.6 = (bf16[8,4096]{1,0:T(8,128)(2,1)S(1)}, bf16[8,4096]{1,0:T(8,128)(2,1)S(1)}, u32[]{:S(2)}, u32[]{:S(2)}) collective-permute-start(bf16[8,4096]{1,0:T(8,128)(2,1)S(1)} %constant_dynamic-update-slice_fusion.2), channel_id=1, source_target_pairs={{0,4},{4,8},{8,12},{12,0},{1,5},{5,9},{9,13},{13,1},{2,6},{6,10},{... | collective-permute-start | bytes 196616 | tf_op jit(solution)/shard_map/ppermute | solution.py:13
  14.8 9.2 %collective-permute-start.3 = (bf16[8,4096]{1,0:T(8,128)(2,1)S(1)}, bf16[8,4096]{1,0:T(8,128)(2,1)S(1)}, u32[]{:S(2)}, u32[]{:S(2)}) collective-permute-start(bf16[8,4096]{1,0:T(8,128)(2,1)S(1)} %convolution_convert_fusion), channel_id=1, source_target_pairs={{0,8},{4,12},{8,0},{12,4},{1,9},{5,13},{9,1},{13,5},{2,10},{6,14},... | collective-permute-start | bytes 196616 | tf_op jit(solution)/shard_map/ppermute | solution.py:13
  17.7 6.3 %collective-permute-start.5 = (bf16[8,4096]{1,0:T(8,128)(2,1)S(1)}, bf16[8,4096]{1,0:T(8,128)(2,1)S(1)}, u32[]{:S(2)}, u32[]{:S(2)}) collective-permute-start(bf16[8,4096]{1,0:T(8,128)(2,1)S(1)} %convolution_convert_fusion), channel_id=1, source_target_pairs={{0,4},{4,8},{8,12},{12,0},{1,5},{5,9},{9,13},{13,1},{2,6},{6,10},{... | collective-permute-start | bytes 196616 | tf_op jit(solution)/shard_map/ppermute | solution.py:13
  32.1 18.3 %collective-permute-start.11 = (bf16[32,3584]{1,0:T(8,128)(2,1)S(1)}, bf16[32,3584]{1,0:T(8,128)(2,1)S(1)}, u32[]{:S(2)}, u32[]{:S(2)}) collective-permute-start(bf16[32,3584]{1,0:T(8,128)(2,1)S(1)} %pad_maximum_fusion.5), channel_id=1, source_target_pairs={{0,1},{1,0},{2,3},{3,2},{4,5},{5,4},{6,7},{7,6},{8,9},{9,8},{10,11... | collective-permute-start | bytes 688136 | tf_op jit(solution)/shard_map/ppermute | solution.py:18
  42.0 10.1 %collective-permute-start.7 = (bf16[32,3584]{1,0:T(8,128)(2,1)S(1)}, bf16[32,3584]{1,0:T(8,128)(2,1)S(1)}, u32[]{:S(2)}, u32[]{:S(2)}) collective-permute-start(bf16[32,3584]{1,0:T(8,128)(2,1)S(1)} %pad_maximum_fusion.3), channel_id=1, source_target_pairs={{0,1},{1,0},{2,3},{3,2},{4,5},{5,4},{6,7},{7,6},{8,9},{9,8},{10,11... | collective-permute-start | bytes 688136 | tf_op jit(solution)/shard_map/ppermute | solution.py:18
  50.4 2.3 %collective-permute-start.9 = (bf16[32,3584]{1,0:T(8,128)(2,1)S(1)}, bf16[32,3584]{1,0:T(8,128)(2,1)S(1)}, u32[]{:S(2)}, u32[]{:S(2)}) collective-permute-start(bf16[32,3584]{1,0:T(8,128)(2,1)S(1)} %pad_maximum_fusion.4), channel_id=1, source_target_pairs={{0,1},{1,0},{2,3},{3,2},{4,5},{5,4},{6,7},{7,6},{8,9},{9,8},{10,11... | collective-permute-start | bytes 688136 | tf_op jit(solution)/shard_map/ppermute | solution.py:18
  50.5 6.1 %collective-permute-start.12 = (bf16[16,3584]{1,0:T(8,128)(2,1)S(1)}, bf16[16,3584]{1,0:T(8,128)(2,1)S(1)}, u32[]{:S(2)}, u32[]{:S(2)}) collective-permute-start(bf16[16,3584]{1,0:T(8,128)(2,1)S(1)} %fusion.9), channel_id=1, source_target_pairs={{0,2},{1,3},{2,0},{3,1},{4,6},{5,7},{6,4},{7,5},{8,10},{9,11},{10,... | collective-permute-start | bytes 344072 | tf_op jit(solution)/shard_map/ppermute | solution.py:18
  52.1 6.9 %collective-permute-start.8 = (bf16[16,3584]{1,0:T(8,128)(2,1)S(1)}, bf16[16,3584]{1,0:T(8,128)(2,1)S(1)}, u32[]{:S(2)}, u32[]{:S(2)}) collective-permute-start(bf16[16,3584]{1,0:T(8,128)(2,1)S(1)} %fusion.17), channel_id=1, source_target_pairs={{0,2},{1,3},{2,0},{3,1},{4,6},{5,7},{6,4},{7,5},{8,10},{9,11},{10,... | collective-permute-start | bytes 344072 | tf_op jit(solution)/shard_map/ppermute | solution.py:18
  52.7 8.3 %collective-permute-start.10 = (bf16[16,3584]{1,0:T(8,128)(2,1)S(1)}, bf16[16,3584]{1,0:T(8,128)(2,1)S(1)}, u32[]{:S(2)}, u32[]{:S(2)}) collective-permute-start(bf16[16,3584]{1,0:T(8,128)(2,1)S(1)} %fusion.11), channel_id=1, source_target_pairs={{0,2},{1,3},{2,0},{3,1},{4,6},{5,7},{6,4},{7,5},{8,10},{9,11},{10,... | collective-permute-start | bytes 344072 | tf_op jit(solution)/shard_map/ppermute | solution.py:18
  61.3 7.2 %collective-permute-start.13 = (bf16[16,7168]{1,0:T(8,128)(2,1)S(1)}, bf16[16,7168]{1,0:T(8,128)(2,1)S(1)}, u32[]{:S(2)}, u32[]{:S(2)}) collective-permute-start(bf16[16,7168]{1,0:T(8,128)(2,1)S(1)} %pad_maximum_fusion.6), channel_id=1, source_target_pairs={{0,2},{1,3},{2,0},{3,1},{4,6},{5,7},{6,4},{7,5},{8,10},{9,11},{10,... | collective-permute-start | bytes 688136 | tf_op jit(solution)/shard_map/ppermute | solution.py:18
  68.5 1.9 %collective-permute-start.14 = (bf16[32,7168]{1,0:T(8,128)(2,1)S(1)}, bf16[32,7168]{1,0:T(8,128)(2,1)S(1)}, u32[]{:S(2)}, u32[]{:S(2)}) collective-permute-start(bf16[32,7168]{1,0:T(8,128)(2,1)S(1)} %pad_maximum_fusion.2), channel_id=1, source_target_pairs={{0,1},{1,0},{2,3},{3,2},{4,5},{5,4},{6,7},{7,6},{8,9},{9,8},{10,11... | collective-permute-start | bytes 1376264 | tf_op jit(solution)/shard_map/ppermute | solution.py:18
  89.9 4.3 %collective-permute-start.15 = (bf16[16,2048]{1,0:T(8,128)(2,1)S(1)}, bf16[16,2048]{1,0:T(8,128)(2,1)S(1)}, u32[]{:S(2)}, u32[]{:S(2)}) collective-permute-start(bf16[16,2048]{1,0:T(8,128)(2,1)S(1)} %get-tuple-element.4), channel_id=1, source_target_pairs={{0,12},{4,0},{8,4},{12,8},{1,13},{5,1},{9,5},{13,9},{2,14},{6,2},{... | collective-permute-start | bytes 196616 | tf_op jit(solution)/shard_map/ppermute | solution.py:13
  91.7 7.4 %collective-permute-start.16 = (bf16[16,2048]{1,0:T(8,128)(2,1)S(1)}, bf16[16,2048]{1,0:T(8,128)(2,1)S(1)}, u32[]{:S(2)}, u32[]{:S(2)}) collective-permute-start(bf16[16,2048]{1,0:T(8,128)(2,1)S(1)} %get-tuple-element.5), channel_id=1, source_target_pairs={{0,8},{4,12},{8,0},{12,4},{1,9},{5,13},{9,1},{13,5},{2,10},{6,14},... | collective-permute-start | bytes 196616 | tf_op jit(solution)/shard_map/ppermute | solution.py:13
  92.1 7.0 %collective-permute-start.17 = (bf16[16,2048]{1,0:T(8,128)(2,1)S(1)}, bf16[16,2048]{1,0:T(8,128)(2,1)S(1)}, u32[]{:S(2)}, u32[]{:S(2)}) collective-permute-start(bf16[16,2048]{1,0:T(8,128)(2,1)S(1)} %get-tuple-element.6), channel_id=1, source_target_pairs={{0,4},{4,8},{8,12},{12,0},{1,5},{5,9},{9,13},{13,1},{2,6},{6,10},{... | collective-permute-start | bytes 196616 | tf_op jit(solution)/shard_map/ppermute | solution.py:13

commit v2 on v0

v2 whole, which is shorter than its diff:
```python
import jax
import jax.numpy as jnp
from jax import lax
from jax.experimental import pallas as pl
from jax.experimental.pallas import tpu as pltpu
from jax.sharding import PartitionSpec as P


F32 = jnp.float32
BF16 = jnp.bfloat16
DIRECT = 4
LIMIT = 6 << 20
CHUNKS = 4
NT = (((1,), (1,)), ((), ()))


def in_vmem(value):
    return pltpu.with_memory_space_constraint(value, pltpu.VMEM)


def in_hbm(value):
    return pltpu.with_memory_space_constraint(value, pltpu.HBM)


def array(shape, dtype):
    return jax.ShapeDtypeStruct(shape, dtype)


def call(kernel, out_shape, values, kinds, flops=0, scratch=(), extra=0):
    memory = {"S": pltpu.SMEM, "V": pltpu.VMEM, "H": pltpu.HBM, "A": pl.ANY}
    values = [in_hbm(v) if kind == "H" else v for v, kind in zip(values, kinds)]
    nbytes = sum(v.size * v.dtype.itemsize for v in values)
    return pl.pallas_call(
        kernel,
        out_shape=out_shape,
        in_specs=[pl.BlockSpec(memory_space=memory[kind]) for kind in kinds],
        out_specs=jax.tree.map(lambda _: pl.BlockSpec(memory_space=pltpu.VMEM), out_shape),
        scratch_shapes=list(scratch),
        compiler_params=pltpu.CompilerParams(vmem_limit_bytes=LIMIT + extra),
        cost_estimate=pl.CostEstimate(flops=max(flops, nbytes), transcendentals=0, bytes_accessed=nbytes),
    )(*values)


def swapped(value, axis, bit):
    size = lax.axis_size(axis)
    return lax.ppermute(value, axis, [(i, i ^ bit) for i in range(size)])


def bits_of(size):
    return [1 << i for i in range(size.bit_length() - 1)]


def blocks_of(rows, count):
    return jnp.split(rows, count, axis=0)


def by_xor(blocks, bits):
    for n, bit in enumerate(bits_of(len(blocks))):
        flip = bits[n : n + 1, :1] != 0
        blocks = [jnp.where(flip, blocks[j ^ bit], blocks[j]) for j in range(len(blocks))]
    return blocks


def gather_rows(value, axis):
    size = lax.axis_size(axis)
    if size > DIRECT:
        return blocks_of(lax.all_gather(value, axis, axis=0, tiled=True), size)
    blocks = [value]
    for k in range(1, size):
        blocks.append(swapped(value, axis, k))
    return blocks


def scatter_rows(blocks, axis):
    size = lax.axis_size(axis)
    if size > DIRECT:
        joined = jnp.concatenate([b.astype(BF16) for b in blocks], axis=0)
        return lax.psum_scatter(joined, axis, scatter_dimension=0, tiled=True).astype(F32)
    total = blocks[0]
    sent = [b.astype(BF16) for b in blocks[1:]]
    for k in range(1, size):
        got = swapped(sent[k - 1], axis, k)
        total = total + got.astype(F32)
    return total


def copies_of(source, target, sems, count=CHUNKS):
    step = source.shape[0] // count
    rows = [pl.ds(i * step, step) for i in range(count)]
    return [pltpu.make_async_copy(source.at[r], target.at[r], sems.at[i]) for i, r in enumerate(rows)]


def loaded(weight, after):
    def kernel(w_ref, after_ref, out_ref, sems):
        copies = copies_of(w_ref, out_ref, sems)
        for copy in copies:
            copy.start()
        for copy in copies:
            copy.wait()

    out = pltpu.VMEM(weight.shape, weight.dtype)
    return call(kernel, out, (weight, after), "HA", int(4e9), [pltpu.SemaphoreType.DMA((CHUNKS,))])


def prepare(flags, image_slots, image_cot, text_rows, text_cot, capacity):
    slots, feat = image_slots.shape
    two = slots == 2 * capacity
    text_dev = text_rows.shape[0]
    kept = capacity if two else slots

    def kernel(flags_ref, slots_ref, cot_ref, text_ref, text_cot_ref, own_ref, give_ref, text_out_ref, bits_ref, sems):
        pairs = []
        for at, image, text in ((pl.ds(0, feat), slots_ref, text_ref), (pl.ds(feat, feat), cot_ref, text_cot_ref)):
            start = flags_ref[0] * capacity if two else 0
            pairs.append((image.at[pl.ds(start, kept)], own_ref.at[:, at]))
            pairs.append((text, text_out_ref.at[:, at]))
            if two:
                pairs.append((image.at[pl.ds(capacity - start, kept)], give_ref.at[:, at]))
        copies = [pltpu.make_async_copy(a, b, sems.at[i]) for i, (a, b) in enumerate(pairs)]
        for copy in copies:
            copy.start()
        row = lax.broadcasted_iota(jnp.int32, bits_ref.shape, 0)
        index = jnp.full(bits_ref.shape, flags_ref[1], jnp.int32)
        bits_ref[...] = lax.shift_right_logical(index, row) & 1
        if not two:
            give_ref[...] = jnp.zeros_like(give_ref)
        for copy in copies:
            copy.wait()

    given = capacity if two else 8
    out = (
        array((kept, 2 * feat), BF16),
        array((given, 2 * feat), BF16),
        array((text_dev, 2 * feat), BF16),
        array((8, 128), jnp.int32),
    )
    values = (flags, image_slots, image_cot, text_rows, text_cot)
    return call(kernel, out, values, "SHHHH", 0, [pltpu.SemaphoreType.DMA((6,))])


def pick(flags, own, got, destination, capacity, two):
    rows = destination.shape[0]
    slots = own.shape[0] * (2 if two else 1)
    width = own.shape[1]

    def kernel(flags_ref, target_ref, own_ref, got_ref, out_ref):
        target = [target_ref[i] for i in range(rows)]
        first = flags_ref[0] if two else 0
        position = lax.broadcasted_iota(jnp.int32, (rows, slots), 0)
        index = lax.broadcasted_iota(jnp.int32, (rows, slots), 1)
        column = jnp.zeros((rows, slots), jnp.int32)
        for i in range(rows):
            rank = jnp.int32(0)
            for j in range(i):
                rank = rank + (target[j] == target[i]).astype(jnp.int32)
            slot = jnp.bitwise_xor(target[i], first) * capacity + rank
            column = jnp.where(position == i, slot, column)
        select = jnp.where(column == index, 1.0, 0.0).astype(BF16)
        if two:
            half = own_ref.shape[0]
            out = jnp.dot(select[:, :half], own_ref[...], preferred_element_type=F32)
            out = out + jnp.dot(select[:, half:], got_ref[...], preferred_element_type=F32)
        else:
            out = jnp.dot(select, own_ref[...], preferred_element_type=F32)
        out_ref[...] = out.astype(BF16)

    return call(kernel, array((rows, width), BF16), (flags, destination, own, got), "SSVV")


def step_of(width):
    for step in (896, 512, 256):
        if width % step == 0:
            return step
    return 128


def split_store(out, keep_ref, give_ref, to, part):
    for i in range(out.shape[0] // part // 2):
        kept = out[2 * i * part : (2 * i + 1) * part]
        given = out[(2 * i + 1) * part : (2 * i + 2) * part]
        keep_ref[i * part : (i + 1) * part, to] = kept
        give_ref[i * part : (i + 1) * part, to] = given.astype(BF16)


def low_part(weight):
    return -(-weight.shape[0] // 256) * 128


def forward_in(x, w_gate, w_up, parts):
    rows = x.shape[0]
    width = w_gate.shape[1]
    step = step_of(width)
    count = width // step

    def kernel(x_ref, gate_ref, up_hbm, keep_ref, give_ref, up_ref, up_sems):
        columns = [pl.ds(j * step, step) for j in range(count)]
        ups = [pltpu.make_async_copy(up_hbm.at[:, c], up_ref.at[:, c], up_sems.at[j]) for j, c in enumerate(columns)]
        for copy in ups:
            copy.start()
        for n, w_ref in enumerate((gate_ref, up_ref)):
            for j, at in enumerate(columns):
                if n == 1:
                    ups[j].wait()
                out = jnp.dot(x_ref[...], w_ref[:, at], preferred_element_type=F32)
                split_store(out, keep_ref, give_ref, pl.ds(n * width + j * step, step), rows // parts)

    out = (
        array((rows // 2, 2 * width), F32),
        array((rows // 2, 2 * width), BF16),
        pltpu.VMEM(w_up.shape, w_up.dtype),
    )
    values = (x, in_vmem(w_gate), w_up)
    scratch = [pltpu.SemaphoreType.DMA((count,))]
    return call(kernel, out, values, "VVH", 4 * rows * w_up.size, scratch)


def forward_back(x, weight, kept, after, parts, first, width):
    rows = x.shape[0]
    step = 256 if width % 256 == 0 else 128
    count = width // step

    def kernel(x_ref, w_ref, after_ref, keep_ref, give_ref, w_buf, sems):
        copies = copies_of(w_ref.at[pl.ds(first, width)], w_buf, sems, count)
        for copy in copies:
            copy.start()
        for j in range(count):
            at = pl.ds(j * step, step)
            copies[j].wait()
            out = lax.dot_general(x_ref[...], w_buf[at, :], NT, preferred_element_type=F32)
            split_store(out, keep_ref, give_ref, at, rows // parts)

    out = (array((rows // 2, width), F32), array((rows // 2, width), BF16))
    scratch = [pltpu.VMEM((width, weight.shape[1]), weight.dtype), pltpu.SemaphoreType.DMA((count,))]
    extra = width * weight.shape[1] * 2
    values = (x, weight, *[w for w in kept[:0]], after)
    return call(kernel, out, values, "VHA", 2 * rows * width * weight.shape[1], scratch, extra)


def halve_first(give, keep, axis):
    half = lax.axis_size(axis) // 2
    got = blocks_of(swapped(give, axis, 1), half)
    return [a + b.astype(F32) for a, b in zip(blocks_of(keep, half), got)]


def sent_rows(blocks):
    return jnp.concatenate([b.astype(BF16) for b in blocks[1::2]], axis=0)


def halve_rest(blocks, axis, sent):
    for bit in bits_of(lax.axis_size(axis))[1:]:
        got = blocks_of(swapped(sent, axis, bit), len(blocks) // 2)
        blocks = [a + b.astype(F32) for a, b in zip(blocks[0::2], got)]
        sent = sent_rows(blocks) if len(blocks) > 1 else None
    return blocks[0]


def double(value, axis):
    pieces = [value]
    for bit in reversed(bits_of(lax.axis_size(axis))):
        got = blocks_of(swapped(jnp.concatenate(pieces, axis=0), axis, bit), len(pieces))
        pieces = [b for pair in zip(pieces, got) for b in pair]
    return pieces


def backward(x, w_gate, w_up):
    rows, _ = x.shape
    feat, hidden = w_gate.shape
    step = min(step_of(feat), 512)

    def kernel(x_ref, gate_ref, up_ref, out_ref):
        for j in range(feat // step):
            at = pl.ds(j * step, step)
            out = lax.dot_general(x_ref[:, :hidden], gate_ref[at, :], NT, preferred_element_type=F32)
            out = out + lax.dot_general(x_ref[:, hidden:], up_ref[at, :], NT, preferred_element_type=F32)
            out_ref[:, at] = out

    values = (x, in_vmem(w_gate), in_vmem(w_up))
    return call(kernel, array((rows, feat), F32), values, "VVV", 4 * rows * w_gate.size)


def per_device(
    image_slots, image_cot, text_rows, text_cot, destination, text_count, w_gate, w_up, w_down
):
    groups = lax.axis_size("group")
    parts = lax.axis_size("dp")
    capacity = image_slots.shape[0] // groups
    image_dev = destination.shape[0]
    feat, hidden = w_gate.shape
    two = groups == 2
    flags = jnp.stack([lax.axis_index("group"), lax.axis_index("dp")]).astype(jnp.int32)
    own, give, text, bits = prepare(flags, image_slots, image_cot, text_rows, text_cot, capacity)
    if two:
        got = swapped(give, "group", 1)
    else:
        own = lax.all_to_all(own, "group", split_axis=0, concat_axis=0, tiled=True)
        got = give
    text_all = gather_rows(text, "tp")
    picked = pick(flags, own, got, destination.reshape(image_dev), capacity, two)
    image_all = gather_rows(picked, "tp")
    w_gate = loaded(w_gate, picked)
    rows = jnp.concatenate([b for pair in zip(image_all, text_all) for b in pair], axis=0)
    rows = jnp.concatenate(by_xor(blocks_of(rows, parts), bits), axis=0)

    keep, give, w_up = forward_in(rows[:, :feat], w_gate, w_up, parts)
    low = low_part(w_down)
    both = halve_first(give, keep, "dp")
    cot = rows[:, feat:]
    sent = sent_rows(both)
    keep_low, give_low = forward_back(cot, w_down, (w_gate, w_up), give, parts, 0, low)
    keep_high, give_high = forward_back(cot, w_down, (w_gate, w_up), sent, parts, low, hidden - low)
    both = halve_rest(both, "dp", sent)
    keep = jnp.concatenate([keep_low, keep_high], axis=1)
    give = jnp.concatenate([give_low, give_high], axis=1)
    back = halve_first(give, keep, "dp")
    back = halve_rest(back, "dp", sent_rows(back))

    gate = both[:, :hidden]
    up = both[:, hidden:]
    sigmoid_gate = jax.nn.sigmoid(gate)
    dgate = (back * up * sigmoid_gate * (1.0 + gate * (1.0 - sigmoid_gate))).astype(BF16)
    dup = (back * gate * sigmoid_gate).astype(BF16)
    spread = by_xor(double(jnp.concatenate([dgate, dup], axis=1), "dp"), bits)
    terms = backward(jnp.concatenate(spread, axis=0), w_gate, w_up)
    grads = scatter_rows(blocks_of(terms, len(image_all)), "tp")
    image_grad = grads[:image_dev].astype(BF16)
    text_part = grads[image_dev:].astype(BF16)
    live = lax.broadcasted_iota(jnp.int32, text_part.shape, 0) < text_count[0]
    text_grad = jnp.where(live, text_part, jnp.zeros_like(text_part))
    return (image_grad, text_grad)


def solution(mesh):
    placed = (
        P(("group", "tp"), "dp"),
        P(("group", "tp"), "dp"),
        P(("group", "tp"), "dp"),
        P(("group", "tp"), "dp"),
        P(("group", "tp"), None),
        P(("group", "tp")),
        P("dp", "tp"),
        P("dp", "tp"),
        P("tp", "dp"),
    )
    return jax.shard_map(
        per_device,
        mesh=mesh,
        in_specs=placed,
        out_specs=(P(("group", "tp"), "dp"), P(("group", "tp"), "dp")),
        check_vma=False,
    )
```

time: 143 us -> 87.6 us (0.61)
  matrix products: 40.7 us -> 0 us
  Pallas kernels: 0 us -> 34.4 us
  blocking collectives: 24.3 us -> 0 us
  waiting for transfers between devices: 50.6 us -> 27.5 us
  starting transfers between devices: 4.28 us -> 19.6 us
  between operations: 14.8 us -> 2.86 us
  other arithmetic: 7.71 us -> 1.61 us
    reduce_scatter x2 -> x0, waiting for transfers between devices: 47.6 us -> none  [the longest x1 27.5 us: language_grads(): lax.psum_scatter(partial_value.astype(jnp.bfloat16), 'dp', scatter_dimens...]
    dot_general x6 -> x0, matrix products: 40.7 us -> none  [the longest x1 10.4 us: language_grads(): lax.dot_general(piece[:, hidden_dev:], w_up, (((1,), (1,)), ((), ())), pr...]
    pallas_call x0 -> x7, Pallas kernels: none -> 34.4 us  [call(): pl.pallas_call(kernel, out_shape=out_shape, in_specs=[pl.BlockSpec(memory...]
    ppermute x0 -> x16, waiting for transfers between devices: none -> 27.5 us  [swapped(): return lax.ppermute(value, axis, [(i, i ^ bit) for i in range(size)])]
    all_gather x2 -> x0, blocking collectives: 24.3 us -> none  [the longest x1 15.6 us: language_grads(): piece = lax.all_gather(combined, 'tp', axis=0, tiled=True)]
    ppermute x0 -> x16, starting transfers between devices: none -> 19.6 us  [swapped(): return lax.ppermute(value, axis, [(i, i ^ bit) for i in range(size)])]
    all_to_all x1 -> x0, starting transfers between devices: 4.23 us -> none  [per_device(): lax.all_to_all(both, 'group', split_axis=0, concat_axis=0, tiled=True)]
    all_to_all x1 -> x0, waiting for transfers between devices: 2.98 us -> none  [per_device(): lax.all_to_all(both, 'group', split_axis=0, concat_axis=0, tiled=True)]
  transfers between devices with their start and end apart: 3 -> 16, of which waited for: 3 -> 10; matrix products, arithmetic and copies ran while one was open for 1% -> 1% of each run, Pallas kernels for 0% -> 14%
where the time goes in v2:
time: 87.6 us; the launch traced here: 87.3 us
  Pallas kernels  34.4 us (39%)
  waiting for transfers between devices  27.5 us (31%)
  starting transfers between devices  19.6 us (22%)
  between operations  2.86 us (3%)
  other arithmetic  1.61 us (2%)
  local copies, waits for them, and re-layouts  1.3 us (1%)
    pallas_call x7, Pallas kernels, call(): pl.pallas_call(kernel, out_shape=out_shape, in_specs=[pl.BlockSpec(memory...  34.4 us
    ppermute x16, waiting for transfers between devices, swapped(): return lax.ppermute(value, axis, [(i, i ^ bit) for i in range(size)])  27.5 us
    ppermute x16, starting transfers between devices, swapped(): return lax.ppermute(value, axis, [(i, i ^ bit) for i in range(size)])  19.6 us
  transfers between devices with their start and end apart: 16, of which 10 were waited for; matrix products, arithmetic and copies ran while one was open for 1% of the time, Pallas kernels for 14%

profile of v2, /device:TPU:0, one launch (start us, length us, event | category | flops | bytes accessed | tf_op | source)
XLA Modules:
  0.0 87.3 jit_solution(17132707824255831575)
XLA Ops:
  0.7 1.4 %shard_map.104 = (bf16[8,4096]{1,0:T(8,128)(2,1)S(1)}, bf16[8,4096]{1,0:T(8,128)(2,1)S(1)}, bf16[8,4096]{1,0:T(8,128)(2,1)S(1)}, s32[8,128]{1,0:T(8,128)S(1)}) custom-call(s32[2]{0:T(128)S(1)} %pad_add_fusion.flags_ref, bf16[16,2048]{1,0:T(8,128)(2,1)} %slots_ref.1, bf16[16,2048]{1,0:T(8,128)(2,1)} %cot_ref.1, bf16[8,2048]{1,0:T(8,128)(2,1)} %text_ref.1, ...), custom_call_target="tpu_custom_call" | custom-call | flops 196616 | bytes 196616 | tf_op jit(solution)/shard_map/pallas_call | solution.py:33
  2.2 3.1 %collective-permute-start.6 = (bf16[8,4096]{1,0:T(8,128)(2,1)S(1)}, bf16[8,4096]{1,0:T(8,128)(2,1)S(1)}, u32[]{:S(2)}, u32[]{:S(2)}) collective-permute-start(bf16[8,4096]{1,0:T(8,128)(2,1)S(1)} %get-tuple-element.16), channel_id=1, source_target_pairs={{0,4},{4,0},{8,12},{12,8},{1,5},{5,1},{9,13},{13,9},{2,6},{6,2},{1... | collective-permute-start | bytes 196616 | tf_op jit(solution)/shard_map/ppermute | solution.py:46
  5.3 2.6 %collective-permute-start.4 = (bf16[8,4096]{1,0:T(8,128)(2,1)S(1)}, bf16[8,4096]{1,0:T(8,128)(2,1)S(1)}, u32[]{:S(2)}, u32[]{:S(2)}) collective-permute-start(bf16[8,4096]{1,0:T(8,128)(2,1)S(1)} %get-tuple-element.16), channel_id=1, source_target_pairs={{0,8},{4,12},{8,0},{12,4},{1,9},{5,13},{9,1},{13,5},{2,10},{6,14},... | collective-permute-start | bytes 196616 | tf_op jit(solution)/shard_map/ppermute | solution.py:46
  7.9 1.7 %collective-permute-start = (bf16[8,4096]{1,0:T(8,128)(2,1)S(1)}, bf16[8,4096]{1,0:T(8,128)(2,1)S(1)}, u32[]{:S(2)}, u32[]{:S(2)}) collective-permute-start(bf16[8,4096]{1,0:T(8,128)(2,1)S(1)} %get-tuple-element.15), channel_id=1, source_target_pairs={{0,16},{16,0},{1,17},{17,1},{2,18},{18,2},{3,19},{19,3},{4,20},{20... | collective-permute-start | bytes 196616 | tf_op jit(solution)/shard_map/ppermute | solution.py:46
  12.8 0.8 shard_map.105.after_ref
  13.6 1.0 %collective-permute-start.5 = (bf16[8,4096]{1,0:T(8,128)(2,1)S(1)}, bf16[8,4096]{1,0:T(8,128)(2,1)S(1)}, u32[]{:S(2)}, u32[]{:S(2)}) collective-permute-start(bf16[8,4096]{1,0:T(8,128)(2,1)S(1)} %shard_map.105.after_ref), channel_id=1, source_target_pairs={{0,4},{4,0},{8,12},{12,8},{1,5},{5,1},{9,13},{13,9},{2,6},{6,2},{1... | collective-permute-start | bytes 196616 | tf_op jit(solution)/shard_map/ppermute | solution.py:46
  14.6 3.5 %collective-permute-start.3 = (bf16[8,4096]{1,0:T(8,128)(2,1)S(1)}, bf16[8,4096]{1,0:T(8,128)(2,1)S(1)}, u32[]{:S(2)}, u32[]{:S(2)}) collective-permute-start(bf16[8,4096]{1,0:T(8,128)(2,1)S(1)} %shard_map.105.after_ref), channel_id=1, source_target_pairs={{0,8},{4,12},{8,0},{12,4},{1,9},{5,13},{9,1},{13,5},{2,10},{6,14},... | collective-permute-start | bytes 196616 | tf_op jit(solution)/shard_map/ppermute | solution.py:46
  18.1 5.3 %shard_map.106.gate_ref = bf16[2048,3584]{1,0:T(8,128)(2,1)S(1)} custom-call(bf16[2048,3584]{1,0:T(8,128)(2,1)} %w_ref.3, bf16[8,4096]{1,0:T(8,128)(2,1)S(1)} %shard_map.105.after_ref), custom_call_target="tpu_custom_call" | custom-call | flops 4000000000 | bytes 14745600 | tf_op jit(solution)/shard_map/pallas_call | solution.py:33
  23.5 6.0 %collective-permute-done.1 = bf16[8,4096]{1,0:T(8,128)(2,1)S(1)} collective-permute-done((bf16[8,4096]{1,0:T(8,128)(2,1)S(1)}, bf16[8,4096]{1,0:T(8,128)(2,1)S(1)}, u32[]{:S(2)}, u32[]{:S(2)}) %collective-permute-start.1) | collective-permute-done | bytes 65568 | tf_op jit(solution)/shard_map/ppermute | solution.py:46
  29.8 6.4 %shard_map.107 = (f32[32,7168]{1,0:T(8,128)S(1)}, bf16[32,7168]{1,0:T(8,128)(2,1)S(1)}, bf16[2048,3584]{1,0:T(8,128)(2,1)S(1)}) custom-call(bf16[64,2048]{1,0:T(8,128)(2,1)S(1)} %get-tuple-element.31.x_ref, bf16[2048,3584]{1,0:T(8,128)(2,1)S(1)} %shard_map.106.gate_ref, bf16[2048,3584]{1,0:T(8,128)(2,1)} %up_hbm.1), custom_call_target="tpu_custom_call" | custom-call | flops 1879048192 | bytes 29622272 | tf_op jit(solution)/shard_map/pallas_call | solution.py:33
  36.3 5.8 %shard_map.108 = (f32[32,1792]{1,0:T(8,128)S(1)}, bf16[32,1792]{1,0:T(8,128)(2,1)S(1)}) custom-call(bf16[64,2048]{1,0:T(8,128)(2,1)S(1)} %get-tuple-element.30.x_ref, bf16[3584,2048]{1,0:T(8,128)(2,1)} %w_ref.5, bf16[32,7168]{1,0:T(8,128)(2,1)S(1)} %get-tuple-element.17.after_ref), custom_call_target="tpu_custom_call" | custom-call | flops 469762048 | bytes 15400960 | tf_op jit(solution)/shard_map/pallas_call | solution.py:33
  42.2 5.8 %shard_map.109 = (f32[32,1792]{1,0:T(8,128)S(1)}, bf16[32,1792]{1,0:T(8,128)(2,1)S(1)}) custom-call(bf16[64,2048]{1,0:T(8,128)(2,1)S(1)} %get-tuple-element.30.x_ref, bf16[3584,2048]{1,0:T(8,128)(2,1)} %w_ref.5, bf16[16,7168]{1,0:T(8,128)(2,1)S(1)} %add_convert_fusion.after_ref), custom_call_target="tpu_custom_call" | custom-call | flops 469762048 | bytes 15171584 | tf_op jit(solution)/shard_map/pallas_call | solution.py:33
  47.9 1.6 %collective-permute-start.10 = (bf16[16,7168]{1,0:T(8,128)(2,1)S(1)}, bf16[16,7168]{1,0:T(8,128)(2,1)S(1)}, u32[]{:S(2)}, u32[]{:S(2)}) collective-permute-start(bf16[16,7168]{1,0:T(8,128)(2,1)S(1)} %add_convert_fusion.after_ref), channel_id=1, source_target_pairs={{0,2},{1,3},{2,0},{3,1},{4,6},{5,7},{6,4},{7,5},{8,10},{9,11},{10,... | collective-permute-start | bytes 688136 | tf_op jit(solution)/shard_map/ppermute | solution.py:46
  49.8 1.3 %collective-permute-done.8 = bf16[32,3584]{1,0:T(8,128)(2,1)S(1)} collective-permute-done((bf16[32,3584]{1,0:T(8,128)(2,1)S(1)}, bf16[32,3584]{1,0:T(8,128)(2,1)S(1)}, u32[]{:S(2)}, u32[]{:S(2)}) %collective-permute-start.8) | collective-permute-done | bytes 229408 | tf_op jit(solution)/shard_map/ppermute | solution.py:46
  51.7 4.8 %collective-permute-done.10 = bf16[16,7168]{1,0:T(8,128)(2,1)S(1)} collective-permute-done((bf16[16,7168]{1,0:T(8,128)(2,1)S(1)}, bf16[16,7168]{1,0:T(8,128)(2,1)S(1)}, u32[]{:S(2)}, u32[]{:S(2)}) %collective-permute-start.10) | collective-permute-done | bytes 229408 | tf_op jit(solution)/shard_map/ppermute | solution.py:46
  56.5 1.9 %collective-permute-done.9 = bf16[16,3584]{1,0:T(8,128)(2,1)S(1)} collective-permute-done((bf16[16,3584]{1,0:T(8,128)(2,1)S(1)}, bf16[16,3584]{1,0:T(8,128)(2,1)S(1)}, u32[]{:S(2)}, u32[]{:S(2)}) %collective-permute-start.9) | collective-permute-done | bytes 114720 | tf_op jit(solution)/shard_map/ppermute | solution.py:46
  58.6 1.6 %collective-permute-start.11 = (bf16[16,7168]{1,0:T(8,128)(2,1)S(1)}, bf16[16,7168]{1,0:T(8,128)(2,1)S(1)}, u32[]{:S(2)}, u32[]{:S(2)}) collective-permute-start(bf16[16,7168]{1,0:T(8,128)(2,1)S(1)} %pad_maximum_fusion.4), channel_id=1, source_target_pairs={{0,2},{1,3},{2,0},{3,1},{4,6},{5,7},{6,4},{7,5},{8,10},{9,11},{10,... | collective-permute-start | bytes 688136 | tf_op jit(solution)/shard_map/ppermute | solution.py:46
  60.2 5.6 %collective-permute-done.11 = bf16[16,7168]{1,0:T(8,128)(2,1)S(1)} collective-permute-done((bf16[16,7168]{1,0:T(8,128)(2,1)S(1)}, bf16[16,7168]{1,0:T(8,128)(2,1)S(1)}, u32[]{:S(2)}, u32[]{:S(2)}) %collective-permute-start.11) | collective-permute-done | bytes 229408 | tf_op jit(solution)/shard_map/ppermute | solution.py:46
  66.6 1.2 %collective-permute-done.12 = bf16[32,7168]{1,0:T(8,128)(2,1)S(1)} collective-permute-done((bf16[32,7168]{1,0:T(8,128)(2,1)S(1)}, bf16[32,7168]{1,0:T(8,128)(2,1)S(1)}, u32[]{:S(2)}, u32[]{:S(2)}) %collective-permute-start.12) | collective-permute-done | bytes 458784 | tf_op jit(solution)/shard_map/ppermute | solution.py:46
  68.1 8.9 %shard_map.110 = f32[64,2048]{1,0:T(8,128)S(1)} custom-call(bf16[64,7168]{1,0:T(8,128)(2,1)S(1)} %pad_maximum_fusion.x_ref, bf16[2048,3584]{1,0:T(8,128)(2,1)S(1)} %shard_map.106.gate_ref, bf16[2048,3584]{1,0:T(8,128)(2,1)S(1)} %get-tuple-element.23.up_ref), custom_call_target="tpu_custom_call" | custom-call | flops 1879048192 | bytes 30277632 | tf_op jit(solution)/shard_map/pallas_call | solution.py:33
  77.2 3.4 %collective-permute-start.14 = (bf16[16,2048]{1,0:T(8,128)(2,1)S(1)}, bf16[16,2048]{1,0:T(8,128)(2,1)S(1)}, u32[]{:S(2)}, u32[]{:S(2)}) collective-permute-start(bf16[16,2048]{1,0:T(8,128)(2,1)S(1)} %get-tuple-element.38), channel_id=1, source_target_pairs={{0,8},{4,12},{8,0},{12,4},{1,9},{5,13},{9,1},{13,5},{2,10},{6,14},... | collective-permute-start | bytes 196616 | tf_op jit(solution)/shard_map/ppermute | solution.py:46
  80.6 0.8 collective-permute-done.13
  81.3 2.6 %collective-permute-done.15 = bf16[16,2048]{1,0:T(8,128)(2,1)S(1)} collective-permute-done((bf16[16,2048]{1,0:T(8,128)(2,1)S(1)}, bf16[16,2048]{1,0:T(8,128)(2,1)S(1)}, u32[]{:S(2)}, u32[]{:S(2)}) %collective-permute-start.15) | collective-permute-done | bytes 65568 | tf_op jit(solution)/shard_map/ppermute | solution.py:46
  83.9 2.7 %collective-permute-done.14 = bf16[16,2048]{1,0:T(8,128)(2,1)S(1)} collective-permute-done((bf16[16,2048]{1,0:T(8,128)(2,1)S(1)}, bf16[16,2048]{1,0:T(8,128)(2,1)S(1)}, u32[]{:S(2)}, u32[]{:S(2)}) %collective-permute-start.14) | collective-permute-done | bytes 65568 | tf_op jit(solution)/shard_map/ppermute | solution.py:46
  (44 shorter events, 4.9 us)
Async XLA Ops:
  2.2 27.4 %collective-permute-start.6 = (bf16[8,4096]{1,0:T(8,128)(2,1)S(1)}, bf16[8,4096]{1,0:T(8,128)(2,1)S(1)}, u32[]{:S(2)}, u32[]{:S(2)}) collective-permute-start(bf16[8,4096]{1,0:T(8,128)(2,1)S(1)} %get-tuple-element.16), channel_id=1, source_target_pairs={{0,4},{4,0},{8,12},{12,8},{1,5},{5,1},{9,13},{13,9},{2,6},{6,2},{1... | collective-permute-start | bytes 196616 | tf_op jit(solution)/shard_map/ppermute | solution.py:46
  5.3 24.3 %collective-permute-start.4 = (bf16[8,4096]{1,0:T(8,128)(2,1)S(1)}, bf16[8,4096]{1,0:T(8,128)(2,1)S(1)}, u32[]{:S(2)}, u32[]{:S(2)}) collective-permute-start(bf16[8,4096]{1,0:T(8,128)(2,1)S(1)} %get-tuple-element.16), channel_id=1, source_target_pairs={{0,8},{4,12},{8,0},{12,4},{1,9},{5,13},{9,1},{13,5},{2,10},{6,14},... | collective-permute-start | bytes 196616 | tf_op jit(solution)/shard_map/ppermute | solution.py:46
  7.9 21.7 %collective-permute-start.2 = (bf16[8,4096]{1,0:T(8,128)(2,1)S(1)}, bf16[8,4096]{1,0:T(8,128)(2,1)S(1)}, u32[]{:S(2)}, u32[]{:S(2)}) collective-permute-start(bf16[8,4096]{1,0:T(8,128)(2,1)S(1)} %get-tuple-element.16), channel_id=1, source_target_pairs={{0,12},{4,8},{8,4},{12,0},{1,13},{5,9},{9,5},{13,1},{2,14},{6,10},... | collective-permute-start | bytes 196616 | tf_op jit(solution)/shard_map/ppermute | solution.py:46
  7.9 4.3 %collective-permute-start = (bf16[8,4096]{1,0:T(8,128)(2,1)S(1)}, bf16[8,4096]{1,0:T(8,128)(2,1)S(1)}, u32[]{:S(2)}, u32[]{:S(2)}) collective-permute-start(bf16[8,4096]{1,0:T(8,128)(2,1)S(1)} %get-tuple-element.15), channel_id=1, source_target_pairs={{0,16},{16,0},{1,17},{17,1},{2,18},{18,2},{3,19},{19,3},{4,20},{20... | collective-permute-start | bytes 196616 | tf_op jit(solution)/shard_map/ppermute | solution.py:46
  12.1 0.7 copy-start
  13.6 9.7 %collective-permute-start.5 = (bf16[8,4096]{1,0:T(8,128)(2,1)S(1)}, bf16[8,4096]{1,0:T(8,128)(2,1)S(1)}, u32[]{:S(2)}, u32[]{:S(2)}) collective-permute-start(bf16[8,4096]{1,0:T(8,128)(2,1)S(1)} %shard_map.105.after_ref), channel_id=1, source_target_pairs={{0,4},{4,0},{8,12},{12,8},{1,5},{5,1},{9,13},{13,9},{2,6},{6,2},{1... | collective-permute-start | bytes 196616 | tf_op jit(solution)/shard_map/ppermute | solution.py:46
  14.6 8.9 %collective-permute-start.3 = (bf16[8,4096]{1,0:T(8,128)(2,1)S(1)}, bf16[8,4096]{1,0:T(8,128)(2,1)S(1)}, u32[]{:S(2)}, u32[]{:S(2)}) collective-permute-start(bf16[8,4096]{1,0:T(8,128)(2,1)S(1)} %shard_map.105.after_ref), channel_id=1, source_target_pairs={{0,8},{4,12},{8,0},{12,4},{1,9},{5,13},{9,1},{13,5},{2,10},{6,14},... | collective-permute-start | bytes 196616 | tf_op jit(solution)/shard_map/ppermute | solution.py:46
  23.4 6.1 %collective-permute-start.1 = (bf16[8,4096]{1,0:T(8,128)(2,1)S(1)}, bf16[8,4096]{1,0:T(8,128)(2,1)S(1)}, u32[]{:S(2)}, u32[]{:S(2)}) collective-permute-start(bf16[8,4096]{1,0:T(8,128)(2,1)S(1)} %shard_map.105.after_ref), channel_id=1, source_target_pairs={{0,12},{4,8},{8,4},{12,0},{1,13},{5,9},{9,5},{13,1},{2,14},{6,10},... | collective-permute-start | bytes 196616 | tf_op jit(solution)/shard_map/ppermute | solution.py:46
  36.2 5.9 %collective-permute-start.7 = (bf16[32,7168]{1,0:T(8,128)(2,1)S(1)}, bf16[32,7168]{1,0:T(8,128)(2,1)S(1)}, u32[]{:S(2)}, u32[]{:S(2)}) collective-permute-start(bf16[32,7168]{1,0:T(8,128)(2,1)S(1)} %get-tuple-element.17.after_ref), channel_id=1, source_target_pairs={{0,1},{1,0},{2,3},{3,2},{4,5},{5,4},{6,7},{7,6},{8,9},{9,8},{10,11... | collective-permute-start | bytes 1376264 | tf_op jit(solution)/shard_map/ppermute | solution.py:46
  47.9 8.5 %collective-permute-start.10 = (bf16[16,7168]{1,0:T(8,128)(2,1)S(1)}, bf16[16,7168]{1,0:T(8,128)(2,1)S(1)}, u32[]{:S(2)}, u32[]{:S(2)}) collective-permute-start(bf16[16,7168]{1,0:T(8,128)(2,1)S(1)} %add_convert_fusion.after_ref), channel_id=1, source_target_pairs={{0,2},{1,3},{2,0},{3,1},{4,6},{5,7},{6,4},{7,5},{8,10},{9,11},{10,... | collective-permute-start | bytes 688136 | tf_op jit(solution)/shard_map/ppermute | solution.py:46
  49.5 1.6 %collective-permute-start.8 = (bf16[32,3584]{1,0:T(8,128)(2,1)S(1)}, bf16[32,3584]{1,0:T(8,128)(2,1)S(1)}, u32[]{:S(2)}, u32[]{:S(2)}) collective-permute-start(bf16[32,3584]{1,0:T(8,128)(2,1)S(1)} %pad_maximum_fusion.3), channel_id=1, source_target_pairs={{0,1},{1,0},{2,3},{3,2},{4,5},{5,4},{6,7},{7,6},{8,9},{9,8},{10,11... | collective-permute-start | bytes 688136 | tf_op jit(solution)/shard_map/ppermute | solution.py:46
  51.1 7.3 %collective-permute-start.9 = (bf16[16,3584]{1,0:T(8,128)(2,1)S(1)}, bf16[16,3584]{1,0:T(8,128)(2,1)S(1)}, u32[]{:S(2)}, u32[]{:S(2)}) collective-permute-start(bf16[16,3584]{1,0:T(8,128)(2,1)S(1)} %fusion.3), channel_id=1, source_target_pairs={{0,2},{1,3},{2,0},{3,1},{4,6},{5,7},{6,4},{7,5},{8,10},{9,11},{10,... | collective-permute-start | bytes 344072 | tf_op jit(solution)/shard_map/ppermute | solution.py:46
  58.6 7.2 %collective-permute-start.11 = (bf16[16,7168]{1,0:T(8,128)(2,1)S(1)}, bf16[16,7168]{1,0:T(8,128)(2,1)S(1)}, u32[]{:S(2)}, u32[]{:S(2)}) collective-permute-start(bf16[16,7168]{1,0:T(8,128)(2,1)S(1)} %pad_maximum_fusion.4), channel_id=1, source_target_pairs={{0,2},{1,3},{2,0},{3,1},{4,6},{5,7},{6,4},{7,5},{8,10},{9,11},{10,... | collective-permute-start | bytes 688136 | tf_op jit(solution)/shard_map/ppermute | solution.py:46
  65.9 1.9 %collective-permute-start.12 = (bf16[32,7168]{1,0:T(8,128)(2,1)S(1)}, bf16[32,7168]{1,0:T(8,128)(2,1)S(1)}, u32[]{:S(2)}, u32[]{:S(2)}) collective-permute-start(bf16[32,7168]{1,0:T(8,128)(2,1)S(1)} %pad_maximum_fusion.2), channel_id=1, source_target_pairs={{0,1},{1,0},{2,3},{3,2},{4,5},{5,4},{6,7},{7,6},{8,9},{9,8},{10,11... | collective-permute-start | bytes 1376264 | tf_op jit(solution)/shard_map/ppermute | solution.py:46
  77.0 4.3 %collective-permute-start.13 = (bf16[16,2048]{1,0:T(8,128)(2,1)S(1)}, bf16[16,2048]{1,0:T(8,128)(2,1)S(1)}, u32[]{:S(2)}, u32[]{:S(2)}) collective-permute-start(bf16[16,2048]{1,0:T(8,128)(2,1)S(1)} %get-tuple-element.36), channel_id=1, source_target_pairs={{0,4},{4,0},{8,12},{12,8},{1,5},{5,1},{9,13},{13,9},{2,6},{6,2},{1... | collective-permute-start | bytes 196616 | tf_op jit(solution)/shard_map/ppermute | solution.py:46
  77.1 6.8 %collective-permute-start.15 = (bf16[16,2048]{1,0:T(8,128)(2,1)S(1)}, bf16[16,2048]{1,0:T(8,128)(2,1)S(1)}, u32[]{:S(2)}, u32[]{:S(2)}) collective-permute-start(bf16[16,2048]{1,0:T(8,128)(2,1)S(1)} %get-tuple-element.37), channel_id=1, source_target_pairs={{0,12},{4,8},{8,4},{12,0},{1,13},{5,9},{9,5},{13,1},{2,14},{6,10},... | collective-permute-start | bytes 196616 | tf_op jit(solution)/shard_map/ppermute | solution.py:46
  77.2 9.4 %collective-permute-start.14 = (bf16[16,2048]{1,0:T(8,128)(2,1)S(1)}, bf16[16,2048]{1,0:T(8,128)(2,1)S(1)}, u32[]{:S(2)}, u32[]{:S(2)}) collective-permute-start(bf16[16,2048]{1,0:T(8,128)(2,1)S(1)} %get-tuple-element.38), channel_id=1, source_target_pairs={{0,8},{4,12},{8,0},{12,4},{1,9},{5,13},{9,1},{13,5},{2,10},{6,14},... | collective-permute-start | bytes 196616 | tf_op jit(solution)/shard_map/ppermute | solution.py:46

commit v3 on v2

--- a/solution.py
+++ b/solution.py
@@ -90,26 +90,31 @@
     return [pltpu.make_async_copy(source.at[r], target.at[r], sems.at[i]) for i, r in enumerate(rows)]
 
 
-def loaded(weight, after):
+def loaded(weight, count, after):
     def kernel(w_ref, after_ref, out_ref, sems):
-        copies = copies_of(w_ref, out_ref, sems)
+        copies = copies_of(w_ref.at[pl.ds(0, count)], out_ref, sems)
         for copy in copies:
             copy.start()
         for copy in copies:
             copy.wait()
 
-    out = pltpu.VMEM(weight.shape, weight.dtype)
+    out = pltpu.VMEM((count, weight.shape[1]), weight.dtype)
     return call(kernel, out, (weight, after), "HA", int(4e9), [pltpu.SemaphoreType.DMA((CHUNKS,))])
 
 
-def prepare(flags, image_slots, image_cot, text_rows, text_cot, capacity):
+def prepare(flags, image_slots, image_cot, text_rows, text_cot, destination, capacity):
     slots, feat = image_slots.shape
     two = slots == 2 * capacity
     text_dev = text_rows.shape[0]
+    rows = destination.shape[0]
     kept = capacity if two else slots
-
-    def kernel(flags_ref, slots_ref, cot_ref, text_ref, text_cot_ref, own_ref, give_ref, text_out_ref, bits_ref, sems):
-        pairs = []
+    width = 2 * kept if two else kept
+
+    def kernel(
+        flags_ref, slots_ref, cot_ref, text_ref, text_cot_ref, target_hbm,
+        own_ref, give_ref, text_out_ref, select_ref, bits_ref, target_ref, sems,
+    ):
+        pairs = [(target_hbm, target_ref)]
         for at, image, text in ((pl.ds(0, feat), slots_ref, text_ref), (pl.ds(feat, feat), cot_ref, text_cot_ref)):
             start = flags_ref[0] * capacity if two else 0
             pairs.append((image.at[pl.ds(start, kept)], own_ref.at[:, at]))
@@ -124,47 +129,50 @@
         bits_ref[...] = lax.shift_right_logical(index, row) & 1
         if not two:
             give_ref[...] = jnp.zeros_like(give_ref)
-        for copy in copies:
-            copy.wait()
-
-    given = capacity if two else 8
-    out = (
-        array((kept, 2 * feat), BF16),
-        array((given, 2 * feat), BF16),
-        array((text_dev, 2 * feat), BF16),
-        array((8, 128), jnp.int32),
-    )
-    values = (flags, image_slots, image_cot, text_rows, text_cot)
-    return call(kernel, out, values, "SHHHH", 0, [pltpu.SemaphoreType.DMA((6,))])
-
-
-def pick(flags, own, got, destination, capacity, two):
-    rows = destination.shape[0]
-    slots = own.shape[0] * (2 if two else 1)
-    width = own.shape[1]
-
-    def kernel(flags_ref, target_ref, own_ref, got_ref, out_ref):
+        copies[0].wait()
         target = [target_ref[i] for i in range(rows)]
         first = flags_ref[0] if two else 0
-        position = lax.broadcasted_iota(jnp.int32, (rows, slots), 0)
-        index = lax.broadcasted_iota(jnp.int32, (rows, slots), 1)
-        column = jnp.zeros((rows, slots), jnp.int32)
+        position = lax.broadcasted_iota(jnp.int32, (rows, width), 0)
+        lane = lax.broadcasted_iota(jnp.int32, (rows, width), 1)
+        column = jnp.zeros((rows, width), jnp.int32)
         for i in range(rows):
             rank = jnp.int32(0)
             for j in range(i):
                 rank = rank + (target[j] == target[i]).astype(jnp.int32)
             slot = jnp.bitwise_xor(target[i], first) * capacity + rank
             column = jnp.where(position == i, slot, column)
-        select = jnp.where(column == index, 1.0, 0.0).astype(BF16)
+        select_ref[...] = jnp.where(column == lane, 1.0, 0.0)
+        for copy in copies[1:]:
+            copy.wait()
+
+    given = capacity if two else 8
+    out = (
+        array((kept, 2 * feat), BF16),
+        array((given, 2 * feat), BF16),
+        array((text_dev, 2 * feat), BF16),
+        array((rows, width), F32),
+        array((8, 128), jnp.int32),
+    )
+    values = (flags, image_slots, image_cot, text_rows, text_cot, destination)
+    scratch = [pltpu.SMEM((rows,), jnp.int32), pltpu.SemaphoreType.DMA((7,))]
+    return call(kernel, out, values, "SHHHHH", 0, scratch)
+
+
+def pick(select, own, got, text, two):
+    rows = select.shape[0]
+    width = own.shape[1]
+
+    def kernel(select_ref, own_ref, got_ref, text_ref, out_ref):
+        select = select_ref[...].astype(BF16)
         if two:
             half = own_ref.shape[0]
             out = jnp.dot(select[:, :half], own_ref[...], preferred_element_type=F32)
             out = out + jnp.dot(select[:, half:], got_ref[...], preferred_element_type=F32)
         else:
             out = jnp.dot(select, own_ref[...], preferred_element_type=F32)
-        out_ref[...] = out.astype(BF16)
-
-    return call(kernel, array((rows, width), BF16), (flags, destination, own, got), "SSVV")
+        out_ref[...] = jnp.concatenate([out.astype(BF16), text_ref[...]], axis=0)
+
+    return call(kernel, array((rows + text.shape[0], width), BF16), (select, own, got, text), "VVVV")
 
 
 def step_of(width):
@@ -183,7 +191,7 @@
 
 
 def low_part(weight):
-    return -(-weight.shape[0] // 256) * 128
+    return -(-weight.shape[0] // 1024) * 512
 
 
 def forward_in(x, w_gate, w_up, parts):
@@ -214,26 +222,35 @@
     return call(kernel, out, values, "VVH", 4 * rows * w_up.size, scratch)
 
 
-def forward_back(x, weight, kept, after, parts, first, width):
+def forward_back(x, weight, after, parts, first, width):
     rows = x.shape[0]
-    step = 256 if width % 256 == 0 else 128
+    step = 512 if width % 512 == 0 else 128
     count = width // step
-
-    def kernel(x_ref, w_ref, after_ref, keep_ref, give_ref, w_buf, sems):
-        copies = copies_of(w_ref.at[pl.ds(first, width)], w_buf, sems, count)
+    streamed = weight.shape[0] != width
+
+    def kernel(x_ref, w_ref, after_ref, keep_ref, give_ref, *scratch):
+        copies = []
+        if streamed:
+            copies = copies_of(w_ref.at[pl.ds(first, width)], *scratch, count)
+            w_ref = scratch[0]
         for copy in copies:
             copy.start()
         for j in range(count):
             at = pl.ds(j * step, step)
-            copies[j].wait()
-            out = lax.dot_general(x_ref[...], w_buf[at, :], NT, preferred_element_type=F32)
+            if streamed:
+                copies[j].wait()
+            out = lax.dot_general(x_ref[...], w_ref[at, :], NT, preferred_element_type=F32)
             split_store(out, keep_ref, give_ref, at, rows // parts)
 
     out = (array((rows // 2, width), F32), array((rows // 2, width), BF16))
-    scratch = [pltpu.VMEM((width, weight.shape[1]), weight.dtype), pltpu.SemaphoreType.DMA((count,))]
-    extra = width * weight.shape[1] * 2
-    values = (x, weight, *[w for w in kept[:0]], after)
-    return call(kernel, out, values, "VHA", 2 * rows * width * weight.shape[1], scratch, extra)
+    scratch = []
+    extra = 0
+    if streamed:
+        scratch = [pltpu.VMEM((width, weight.shape[1]), weight.dtype), pltpu.SemaphoreType.DMA((count,))]
+        extra = width * weight.shape[1] * 2
+    values = (x, weight if streamed else in_vmem(weight), after)
+    flops = 2 * rows * width * weight.shape[1]
+    return call(kernel, out, values, "VHA" if streamed else "VVA", flops, scratch, extra)
 
 
 def halve_first(give, keep, axis):
@@ -262,20 +279,21 @@
     return pieces
 
 
-def backward(x, w_gate, w_up):
-    rows, _ = x.shape
-    feat, hidden = w_gate.shape
-    step = min(step_of(feat), 512)
-
-    def kernel(x_ref, gate_ref, up_ref, out_ref):
+def backward(x, weight, added=None):
+    rows = x.shape[0]
+    feat = weight.shape[0]
+    step = 512 if feat % 512 == 0 else 128
+    more = 0 if added is None else 1
+
+    def kernel(x_ref, w_ref, *refs):
+        out_ref = refs[more]
         for j in range(feat // step):
             at = pl.ds(j * step, step)
-            out = lax.dot_general(x_ref[:, :hidden], gate_ref[at, :], NT, preferred_element_type=F32)
-            out = out + lax.dot_general(x_ref[:, hidden:], up_ref[at, :], NT, preferred_element_type=F32)
-            out_ref[:, at] = out
-
-    values = (x, in_vmem(w_gate), in_vmem(w_up))
-    return call(kernel, array((rows, feat), F32), values, "VVV", 4 * rows * w_gate.size)
+            out = lax.dot_general(x_ref[...], w_ref[at, :], NT, preferred_element_type=F32)
+            out_ref[:, at] = out + refs[0][:, at] if more else out
+
+    values = (x, in_vmem(weight), *([added] * more))
+    return call(kernel, array((rows, feat), F32), values, "VV" + "V" * more, 2 * rows * weight.size)
 
 
 def per_device(
@@ -288,26 +306,27 @@
     feat, hidden = w_gate.shape
     two = groups == 2
     flags = jnp.stack([lax.axis_index("group"), lax.axis_index("dp")]).astype(jnp.int32)
-    own, give, text, bits = prepare(flags, image_slots, image_cot, text_rows, text_cot, capacity)
+    target = destination.reshape(image_dev)
+    own, give, text, select, bits = prepare(flags, image_slots, image_cot, text_rows, text_cot, target, capacity)
     if two:
         got = swapped(give, "group", 1)
     else:
         own = lax.all_to_all(own, "group", split_axis=0, concat_axis=0, tiled=True)
         got = give
-    text_all = gather_rows(text, "tp")
-    picked = pick(flags, own, got, destination.reshape(image_dev), capacity, two)
-    image_all = gather_rows(picked, "tp")
-    w_gate = loaded(w_gate, picked)
-    rows = jnp.concatenate([b for pair in zip(image_all, text_all) for b in pair], axis=0)
+    low = low_part(w_down)
+    picked = pick(select, own, got, text, two)
+    gathered = gather_rows(picked, "tp")
+    w_gate = loaded(w_gate, w_gate.shape[0], picked)
+    down_low = loaded(w_down, low, picked)
+    rows = jnp.concatenate(gathered, axis=0)
     rows = jnp.concatenate(by_xor(blocks_of(rows, parts), bits), axis=0)
 
     keep, give, w_up = forward_in(rows[:, :feat], w_gate, w_up, parts)
-    low = low_part(w_down)
     both = halve_first(give, keep, "dp")
     cot = rows[:, feat:]
     sent = sent_rows(both)
-    keep_low, give_low = forward_back(cot, w_down, (w_gate, w_up), give, parts, 0, low)
-    keep_high, give_high = forward_back(cot, w_down, (w_gate, w_up), sent, parts, low, hidden - low)
+    keep_low, give_low = forward_back(cot, down_low, give, parts, 0, low)
+    keep_high, give_high = forward_back(cot, w_down, sent, parts, low, hidden - low)
     both = halve_rest(both, "dp", sent)
     keep = jnp.concatenate([keep_low, keep_high], axis=1)
     give = jnp.concatenate([give_low, give_high], axis=1)
@@ -319,9 +338,11 @@
     sigmoid_gate = jax.nn.sigmoid(gate)
     dgate = (back * up * sigmoid_gate * (1.0 + gate * (1.0 - sigmoid_gate))).astype(BF16)
     dup = (back * gate * sigmoid_gate).astype(BF16)
-    spread = by_xor(double(jnp.concatenate([dgate, dup], axis=1), "dp"), bits)
-    terms = backward(jnp.concatenate(spread, axis=0), w_gate, w_up)
-    grads = scatter_rows(blocks_of(terms, len(image_all)), "tp")
+    spread_gate = by_xor(double(dgate, "dp"), bits)
+    spread_up = by_xor(double(dup, "dp"), bits)
+    terms = backward(jnp.concatenate(spread_gate, axis=0), w_gate)
+    terms = backward(jnp.concatenate(spread_up, axis=0), w_up, terms)
+    grads = scatter_rows(blocks_of(terms, len(gathered)), "tp")
     image_grad = grads[:image_dev].astype(BF16)
     text_part = grads[image_dev:].astype(BF16)
     live = lax.broadcasted_iota(jnp.int32, text_part.shape, 0) < text_count[0]

time: 87.6 us -> 73.7 us (0.84)
  waiting for transfers between devices: 27.5 us -> 19.1 us
  starting transfers between devices: 19.6 us -> 17.1 us
  Pallas kernels: 34.4 us -> 32.4 us
    ppermute x16 -> x15, waiting for transfers between devices: 27.5 us -> 19.1 us  [swapped(): return lax.ppermute(value, axis, [(i, i ^ bit) for i in range(size)])]
    ppermute x16 -> x15, starting transfers between devices: 19.6 us -> 17.1 us  [swapped(): return lax.ppermute(value, axis, [(i, i ^ bit) for i in range(size)])]
    pallas_call x7 -> x9, Pallas kernels: 34.4 us -> 32.4 us  [call(): pl.pallas_call(kernel, out_shape=out_shape, in_specs=[pl.BlockSpec(memory...]
  transfers between devices with their start and end apart: 16 -> 15, of which waited for: 10 -> 10; matrix products, arithmetic and copies ran while one was open for 1% -> 1% of each run, Pallas kernels for 14% -> 27%
where the time goes in v3:
time: 73.7 us; the launch traced here: 73.5 us
  Pallas kernels  32.4 us (44%)
  waiting for transfers between devices  19.1 us (26%)
  starting transfers between devices  17.1 us (23%)
  between operations  2.82 us (4%)
  other arithmetic  1.43 us (2%)
    pallas_call x9, Pallas kernels, call(): pl.pallas_call(kernel, out_shape=out_shape, in_specs=[pl.BlockSpec(memory...  32.4 us
    ppermute x15, waiting for transfers between devices, swapped(): return lax.ppermute(value, axis, [(i, i ^ bit) for i in range(size)])  19.1 us
    ppermute x15, starting transfers between devices, swapped(): return lax.ppermute(value, axis, [(i, i ^ bit) for i in range(size)])  17.1 us
  transfers between devices with their start and end apart: 15, of which 10 were waited for; matrix products, arithmetic and copies ran while one was open for 1% of the time, Pallas kernels for 27%

profile of v3, /device:TPU:0, one launch (start us, length us, event | category | flops | bytes accessed | tf_op | source)
XLA Modules:
  0.0 73.5 jit_solution(16628014214857743308)
XLA Ops:
  0.7 1.4 %shard_map.104 = (bf16[8,4096]{1,0:T(8,128)(2,1)S(1)}, bf16[8,4096]{1,0:T(8,128)(2,1)S(1)}, bf16[8,4096]{1,0:T(8,128)(2,1)S(1)}, f32[8,16]{1,0:T(8,128)S(1)}, s32[8,128]{1,0:T(8,128)S(1)}) custom-call(s32[2]{0:T(128)S(1)} %pad_add_fusion.flags_ref, bf16[16,2048]{1,0:T(8,128)(2,1)} %slots_ref.1, bf16[16,2048]{1,0:T(8,128)(2,1)} %cot_ref.1, ...), custom_call_target="tpu_custom_call" | custom-call | flops 196648 | bytes 196648 | tf_op jit(solution)/shard_map/pallas_call | solution.py:33
  2.2 3.0 %collective-permute-start = (bf16[8,4096]{1,0:T(8,128)(2,1)S(1)}, bf16[8,4096]{1,0:T(8,128)(2,1)S(1)}, u32[]{:S(2)}, u32[]{:S(2)}) collective-permute-start(bf16[8,4096]{1,0:T(8,128)(2,1)S(1)} %get-tuple-element.17), channel_id=1, source_target_pairs={{0,16},{16,0},{1,17},{17,1},{2,18},{18,2},{3,19},{19,3},{4,20},{20... | collective-permute-start | bytes 196616 | tf_op jit(solution)/shard_map/ppermute | solution.py:46
  7.7 4.2 %collective-permute-start.1 = (bf16[16,4096]{1,0:T(8,128)(2,1)S(1)}, bf16[16,4096]{1,0:T(8,128)(2,1)S(1)}, u32[]{:S(2)}, u32[]{:S(2)}) collective-permute-start(bf16[16,4096]{1,0:T(8,128)(2,1)S(1)} %shard_map.105.after_ref), channel_id=1, source_target_pairs={{0,12},{4,8},{8,4},{12,0},{1,13},{5,9},{9,5},{13,1},{2,14},{6,10},... | collective-permute-start | bytes 393224 | tf_op jit(solution)/shard_map/ppermute | solution.py:46
  11.9 0.6 collective-permute-start.3
  12.6 5.3 %shard_map.107.gate_ref.w_ref = bf16[2048,3584]{1,0:T(8,128)(2,1)S(1)} custom-call(bf16[2048,3584]{1,0:T(8,128)(2,1)} %w_ref.4, bf16[16,4096]{1,0:T(8,128)(2,1)S(1)} %shard_map.105.after_ref), custom_call_target="tpu_custom_call" | custom-call | flops 4000000000 | bytes 14811136 | tf_op jit(solution)/shard_map/pallas_call | solution.py:33
  17.8 4.0 %collective-permute-done.2 = bf16[16,4096]{1,0:T(8,128)(2,1)S(1)} collective-permute-done((bf16[16,4096]{1,0:T(8,128)(2,1)S(1)}, bf16[16,4096]{1,0:T(8,128)(2,1)S(1)}, u32[]{:S(2)}, u32[]{:S(2)}) %collective-permute-start.2) | collective-permute-done | bytes 131104 | tf_op jit(solution)/shard_map/ppermute | solution.py:46
  22.0 6.4 %shard_map.108 = (f32[32,7168]{1,0:T(8,128)S(1)}, bf16[32,7168]{1,0:T(8,128)(2,1)S(1)}, bf16[2048,3584]{1,0:T(8,128)(2,1)S(1)}) custom-call(bf16[64,2048]{1,0:T(8,128)(2,1)S(1)} %get-tuple-element.29.x_ref, bf16[2048,3584]{1,0:T(8,128)(2,1)S(1)} %shard_map.107.gate_ref.w_ref, bf16[2048,3584]{1,0:T(8,128)(2,1)} %up_hbm.1), custom_call_target="tpu_custom_call" | custom-call | flops 1879048192 | bytes 29622272 | tf_op jit(solution)/shard_map/pallas_call | solution.py:33
  28.4 3.5 %shard_map.106.w_ref = bf16[2048,2048]{1,0:T(8,128)(2,1)S(1)} custom-call(bf16[3584,2048]{1,0:T(8,128)(2,1)} %w_ref.5, bf16[16,4096]{1,0:T(8,128)(2,1)S(1)} %shard_map.105.after_ref), custom_call_target="tpu_custom_call" | custom-call | flops 4000000000 | bytes 14811136 | tf_op jit(solution)/shard_map/pallas_call | solution.py:33
  32.0 2.6 %shard_map.109 = (f32[32,2048]{1,0:T(8,128)S(1)}, bf16[32,2048]{1,0:T(8,128)(2,1)S(1)}) custom-call(bf16[64,2048]{1,0:T(8,128)(2,1)S(1)} %get-tuple-element.28.x_ref, bf16[2048,2048]{1,0:T(8,128)(2,1)S(1)} %shard_map.106.w_ref, bf16[32,7168]{1,0:T(8,128)(2,1)S(1)} %get-tuple-element.19.after_ref), custom_call_target="tpu_custom_call" | custom-call | flops 536870912 | bytes 9109504 | tf_op jit(solution)/shard_map/pallas_call | solution.py:33
  34.7 1.6 %collective-permute-start.7 = (bf16[16,7168]{1,0:T(8,128)(2,1)S(1)}, bf16[16,7168]{1,0:T(8,128)(2,1)S(1)}, u32[]{:S(2)}, u32[]{:S(2)}) collective-permute-start(bf16[16,7168]{1,0:T(8,128)(2,1)S(1)} %add_convert_fusion.after_ref), channel_id=1, source_target_pairs={{0,2},{1,3},{2,0},{3,1},{4,6},{5,7},{6,4},{7,5},{8,10},{9,11},{10,... | collective-permute-start | bytes 688136 | tf_op jit(solution)/shard_map/ppermute | solution.py:46
  36.3 3.9 %shard_map.110 = (f32[32,1536]{1,0:T(8,128)S(1)}, bf16[32,1536]{1,0:T(8,128)(2,1)S(1)}) custom-call(bf16[64,2048]{1,0:T(8,128)(2,1)S(1)} %get-tuple-element.28.x_ref, bf16[3584,2048]{1,0:T(8,128)(2,1)} %w_ref.5, bf16[16,7168]{1,0:T(8,128)(2,1)S(1)} %add_convert_fusion.after_ref), custom_call_target="tpu_custom_call" | custom-call | flops 402653184 | bytes 15171584 | tf_op jit(solution)/shard_map/pallas_call | solution.py:33
  40.5 1.3 %collective-permute-done.5 = bf16[32,3584]{1,0:T(8,128)(2,1)S(1)} collective-permute-done((bf16[32,3584]{1,0:T(8,128)(2,1)S(1)}, bf16[32,3584]{1,0:T(8,128)(2,1)S(1)}, u32[]{:S(2)}, u32[]{:S(2)}) %collective-permute-start.5) | collective-permute-done | bytes 229408 | tf_op jit(solution)/shard_map/ppermute | solution.py:46
  41.8 0.6 collective-permute-start.6
  42.8 4.3 %collective-permute-done.6 = bf16[16,3584]{1,0:T(8,128)(2,1)S(1)} collective-permute-done((bf16[16,3584]{1,0:T(8,128)(2,1)S(1)}, bf16[16,3584]{1,0:T(8,128)(2,1)S(1)}, u32[]{:S(2)}, u32[]{:S(2)}) %collective-permute-start.6) | collective-permute-done | bytes 114720 | tf_op jit(solution)/shard_map/ppermute | solution.py:46
  48.5 1.6 %collective-permute-start.8 = (bf16[16,3584]{1,0:T(8,128)(2,1)S(1)}, bf16[16,3584]{1,0:T(8,128)(2,1)S(1)}, u32[]{:S(2)}, u32[]{:S(2)}) collective-permute-start(bf16[16,3584]{1,0:T(8,128)(2,1)S(1)} %get-tuple-element.27), channel_id=1, source_target_pairs={{0,2},{1,3},{2,0},{3,1},{4,6},{5,7},{6,4},{7,5},{8,10},{9,11},{10,... | collective-permute-start | bytes 344072 | tf_op jit(solution)/shard_map/ppermute | solution.py:46
  50.1 2.9 %collective-permute-done.10 = bf16[16,3584]{1,0:T(8,128)(2,1)S(1)} collective-permute-done((bf16[16,3584]{1,0:T(8,128)(2,1)S(1)}, bf16[16,3584]{1,0:T(8,128)(2,1)S(1)}, u32[]{:S(2)}, u32[]{:S(2)}) %collective-permute-start.10) | collective-permute-done | bytes 114720 | tf_op jit(solution)/shard_map/ppermute | solution.py:46
  53.0 1.1 %collective-permute-done.8 = bf16[16,3584]{1,0:T(8,128)(2,1)S(1)} collective-permute-done((bf16[16,3584]{1,0:T(8,128)(2,1)S(1)}, bf16[16,3584]{1,0:T(8,128)(2,1)S(1)}, u32[]{:S(2)}, u32[]{:S(2)}) %collective-permute-start.8) | collective-permute-done | bytes 114720 | tf_op jit(solution)/shard_map/ppermute | solution.py:46
  54.6 4.5 %shard_map.111.refs_0_ = f32[64,2048]{1,0:T(8,128)S(1)} custom-call(bf16[64,3584]{1,0:T(8,128)(2,1)S(1)} %pad_maximum_fusion.2.x_ref, bf16[2048,3584]{1,0:T(8,128)(2,1)S(1)} %shard_map.107.gate_ref.w_ref), custom_call_target="tpu_custom_call" | custom-call | flops 939524096 | bytes 15138816 | tf_op jit(solution)/shard_map/pallas_call | solution.py:33
  59.2 4.5 %shard_map.112 = f32[64,2048]{1,0:T(8,128)S(1)} custom-call(bf16[64,3584]{1,0:T(8,128)(2,1)S(1)} %pad_maximum_fusion.1.x_ref, bf16[2048,3584]{1,0:T(8,128)(2,1)S(1)} %get-tuple-element.25.w_ref, f32[64,2048]{1,0:T(8,128)S(1)} %shard_map.111.refs_0_), custom_call_target="tpu_custom_call" | custom-call | flops 939524096 | bytes 15663104 | tf_op jit(solution)/shard_map/pallas_call | solution.py:33
  63.8 2.6 %collective-permute-start.14 = (bf16[16,2048]{1,0:T(8,128)(2,1)S(1)}, bf16[16,2048]{1,0:T(8,128)(2,1)S(1)}, u32[]{:S(2)}, u32[]{:S(2)}) collective-permute-start(bf16[16,2048]{1,0:T(8,128)(2,1)S(1)} %get-tuple-element.43), channel_id=1, source_target_pairs={{0,12},{4,8},{8,4},{12,0},{1,13},{5,9},{9,5},{13,1},{2,14},{6,10},... | collective-permute-start | bytes 196616 | tf_op jit(solution)/shard_map/ppermute | solution.py:46
  66.4 1.9 %collective-permute-start.12 = (bf16[16,2048]{1,0:T(8,128)(2,1)S(1)}, bf16[16,2048]{1,0:T(8,128)(2,1)S(1)}, u32[]{:S(2)}, u32[]{:S(2)}) collective-permute-start(bf16[16,2048]{1,0:T(8,128)(2,1)S(1)} %get-tuple-element.42), channel_id=1, source_target_pairs={{0,4},{4,0},{8,12},{12,8},{1,5},{5,1},{9,13},{13,9},{2,6},{6,2},{1... | collective-permute-start | bytes 196616 | tf_op jit(solution)/shard_map/ppermute | solution.py:46
  68.3 2.4 %collective-permute-done.14 = bf16[16,2048]{1,0:T(8,128)(2,1)S(1)} collective-permute-done((bf16[16,2048]{1,0:T(8,128)(2,1)S(1)}, bf16[16,2048]{1,0:T(8,128)(2,1)S(1)}, u32[]{:S(2)}, u32[]{:S(2)}) %collective-permute-start.14) | collective-permute-done | bytes 65568 | tf_op jit(solution)/shard_map/ppermute | solution.py:46
  70.7 2.0 %collective-permute-done.13 = bf16[16,2048]{1,0:T(8,128)(2,1)S(1)} collective-permute-done((bf16[16,2048]{1,0:T(8,128)(2,1)S(1)}, bf16[16,2048]{1,0:T(8,128)(2,1)S(1)}, u32[]{:S(2)}, u32[]{:S(2)}) %collective-permute-start.13) | collective-permute-done | bytes 65568 | tf_op jit(solution)/shard_map/ppermute | solution.py:46
  72.8 0.7 slice_select_fusion
  (38 shorter events, 3.7 us)
Async XLA Ops:
  2.2 5.3 %collective-permute-start = (bf16[8,4096]{1,0:T(8,128)(2,1)S(1)}, bf16[8,4096]{1,0:T(8,128)(2,1)S(1)}, u32[]{:S(2)}, u32[]{:S(2)}) collective-permute-start(bf16[8,4096]{1,0:T(8,128)(2,1)S(1)} %get-tuple-element.17), channel_id=1, source_target_pairs={{0,16},{16,0},{1,17},{17,1},{2,18},{18,2},{3,19},{19,3},{4,20},{20... | collective-permute-start | bytes 196616 | tf_op jit(solution)/shard_map/ppermute | solution.py:46
  7.7 10.1 %collective-permute-start.1 = (bf16[16,4096]{1,0:T(8,128)(2,1)S(1)}, bf16[16,4096]{1,0:T(8,128)(2,1)S(1)}, u32[]{:S(2)}, u32[]{:S(2)}) collective-permute-start(bf16[16,4096]{1,0:T(8,128)(2,1)S(1)} %shard_map.105.after_ref), channel_id=1, source_target_pairs={{0,12},{4,8},{8,4},{12,0},{1,13},{5,9},{9,5},{13,1},{2,14},{6,10},... | collective-permute-start | bytes 393224 | tf_op jit(solution)/shard_map/ppermute | solution.py:46
  11.9 9.9 %collective-permute-start.2 = (bf16[16,4096]{1,0:T(8,128)(2,1)S(1)}, bf16[16,4096]{1,0:T(8,128)(2,1)S(1)}, u32[]{:S(2)}, u32[]{:S(2)}) collective-permute-start(bf16[16,4096]{1,0:T(8,128)(2,1)S(1)} %shard_map.105.after_ref), channel_id=1, source_target_pairs={{0,8},{4,12},{8,0},{12,4},{1,9},{5,13},{9,1},{13,5},{2,10},{6,14},... | collective-permute-start | bytes 393224 | tf_op jit(solution)/shard_map/ppermute | solution.py:46
  11.9 9.9 %collective-permute-start.3 = (bf16[16,4096]{1,0:T(8,128)(2,1)S(1)}, bf16[16,4096]{1,0:T(8,128)(2,1)S(1)}, u32[]{:S(2)}, u32[]{:S(2)}) collective-permute-start(bf16[16,4096]{1,0:T(8,128)(2,1)S(1)} %shard_map.105.after_ref), channel_id=1, source_target_pairs={{0,4},{4,0},{8,12},{12,8},{1,5},{5,1},{9,13},{13,9},{2,6},{6,2},{1... | collective-permute-start | bytes 393224 | tf_op jit(solution)/shard_map/ppermute | solution.py:46
  28.4 6.3 %collective-permute-start.4 = (bf16[32,7168]{1,0:T(8,128)(2,1)S(1)}, bf16[32,7168]{1,0:T(8,128)(2,1)S(1)}, u32[]{:S(2)}, u32[]{:S(2)}) collective-permute-start(bf16[32,7168]{1,0:T(8,128)(2,1)S(1)} %get-tuple-element.19.after_ref), channel_id=1, source_target_pairs={{0,1},{1,0},{2,3},{3,2},{4,5},{5,4},{6,7},{7,6},{8,9},{9,8},{10,11... | collective-permute-start | bytes 1376264 | tf_op jit(solution)/shard_map/ppermute | solution.py:46
  34.7 8.1 %collective-permute-start.7 = (bf16[16,7168]{1,0:T(8,128)(2,1)S(1)}, bf16[16,7168]{1,0:T(8,128)(2,1)S(1)}, u32[]{:S(2)}, u32[]{:S(2)}) collective-permute-start(bf16[16,7168]{1,0:T(8,128)(2,1)S(1)} %add_convert_fusion.after_ref), channel_id=1, source_target_pairs={{0,2},{1,3},{2,0},{3,1},{4,6},{5,7},{6,4},{7,5},{8,10},{9,11},{10,... | collective-permute-start | bytes 688136 | tf_op jit(solution)/shard_map/ppermute | solution.py:46
  40.2 1.6 %collective-permute-start.5 = (bf16[32,3584]{1,0:T(8,128)(2,1)S(1)}, bf16[32,3584]{1,0:T(8,128)(2,1)S(1)}, u32[]{:S(2)}, u32[]{:S(2)}) collective-permute-start(bf16[32,3584]{1,0:T(8,128)(2,1)S(1)} %pad_maximum_fusion.3), channel_id=1, source_target_pairs={{0,1},{1,0},{2,3},{3,2},{4,5},{5,4},{6,7},{7,6},{8,9},{9,8},{10,11... | collective-permute-start | bytes 688136 | tf_op jit(solution)/shard_map/ppermute | solution.py:46
  41.8 5.3 %collective-permute-start.6 = (bf16[16,3584]{1,0:T(8,128)(2,1)S(1)}, bf16[16,3584]{1,0:T(8,128)(2,1)S(1)}, u32[]{:S(2)}, u32[]{:S(2)}) collective-permute-start(bf16[16,3584]{1,0:T(8,128)(2,1)S(1)} %fusion.3), channel_id=1, source_target_pairs={{0,2},{1,3},{2,0},{3,1},{4,6},{5,7},{6,4},{7,5},{8,10},{9,11},{10,... | collective-permute-start | bytes 344072 | tf_op jit(solution)/shard_map/ppermute | solution.py:46
  47.3 5.7 %collective-permute-start.10 = (bf16[16,3584]{1,0:T(8,128)(2,1)S(1)}, bf16[16,3584]{1,0:T(8,128)(2,1)S(1)}, u32[]{:S(2)}, u32[]{:S(2)}) collective-permute-start(bf16[16,3584]{1,0:T(8,128)(2,1)S(1)} %get-tuple-element.26), channel_id=1, source_target_pairs={{0,2},{1,3},{2,0},{3,1},{4,6},{5,7},{6,4},{7,5},{8,10},{9,11},{10,... | collective-permute-start | bytes 344072 | tf_op jit(solution)/shard_map/ppermute | solution.py:46
  48.5 5.7 %collective-permute-start.8 = (bf16[16,3584]{1,0:T(8,128)(2,1)S(1)}, bf16[16,3584]{1,0:T(8,128)(2,1)S(1)}, u32[]{:S(2)}, u32[]{:S(2)}) collective-permute-start(bf16[16,3584]{1,0:T(8,128)(2,1)S(1)} %get-tuple-element.27), channel_id=1, source_target_pairs={{0,2},{1,3},{2,0},{3,1},{4,6},{5,7},{6,4},{7,5},{8,10},{9,11},{10,... | collective-permute-start | bytes 344072 | tf_op jit(solution)/shard_map/ppermute | solution.py:46
  53.0 1.6 %collective-permute-start.11 = (bf16[32,3584]{1,0:T(8,128)(2,1)S(1)}, bf16[32,3584]{1,0:T(8,128)(2,1)S(1)}, u32[]{:S(2)}, u32[]{:S(2)}) collective-permute-start(bf16[32,3584]{1,0:T(8,128)(2,1)S(1)} %pad_maximum_fusion.5), channel_id=1, source_target_pairs={{0,1},{1,0},{2,3},{3,2},{4,5},{5,4},{6,7},{7,6},{8,9},{9,8},{10,11... | collective-permute-start | bytes 688136 | tf_op jit(solution)/shard_map/ppermute | solution.py:46
  54.2 4.9 %collective-permute-start.9 = (bf16[32,3584]{1,0:T(8,128)(2,1)S(1)}, bf16[32,3584]{1,0:T(8,128)(2,1)S(1)}, u32[]{:S(2)}, u32[]{:S(2)}) collective-permute-start(bf16[32,3584]{1,0:T(8,128)(2,1)S(1)} %pad_maximum_fusion.4), channel_id=1, source_target_pairs={{0,1},{1,0},{2,3},{3,2},{4,5},{5,4},{6,7},{7,6},{8,9},{9,8},{10,11... | collective-permute-start | bytes 688136 | tf_op jit(solution)/shard_map/ppermute | solution.py:46
  63.8 6.9 %collective-permute-start.14 = (bf16[16,2048]{1,0:T(8,128)(2,1)S(1)}, bf16[16,2048]{1,0:T(8,128)(2,1)S(1)}, u32[]{:S(2)}, u32[]{:S(2)}) collective-permute-start(bf16[16,2048]{1,0:T(8,128)(2,1)S(1)} %get-tuple-element.43), channel_id=1, source_target_pairs={{0,12},{4,8},{8,4},{12,0},{1,13},{5,9},{9,5},{13,1},{2,14},{6,10},... | collective-permute-start | bytes 196616 | tf_op jit(solution)/shard_map/ppermute | solution.py:46
  66.3 6.4 %collective-permute-start.13 = (bf16[16,2048]{1,0:T(8,128)(2,1)S(1)}, bf16[16,2048]{1,0:T(8,128)(2,1)S(1)}, u32[]{:S(2)}, u32[]{:S(2)}) collective-permute-start(bf16[16,2048]{1,0:T(8,128)(2,1)S(1)} %get-tuple-element.44), channel_id=1, source_target_pairs={{0,8},{4,12},{8,0},{12,4},{1,9},{5,13},{9,1},{13,5},{2,10},{6,14},... | collective-permute-start | bytes 196616 | tf_op jit(solution)/shard_map/ppermute | solution.py:46
  66.4 6.4 %collective-permute-start.12 = (bf16[16,2048]{1,0:T(8,128)(2,1)S(1)}, bf16[16,2048]{1,0:T(8,128)(2,1)S(1)}, u32[]{:S(2)}, u32[]{:S(2)}) collective-permute-start(bf16[16,2048]{1,0:T(8,128)(2,1)S(1)} %get-tuple-element.42), channel_id=1, source_target_pairs={{0,4},{4,0},{8,12},{12,8},{1,5},{5,1},{9,13},{13,9},{2,6},{6,2},{1... | collective-permute-start | bytes 196616 | tf_op jit(solution)/shard_map/ppermute | solution.py:46

commit v4 on v3

--- a/solution.py
+++ b/solution.py
@@ -102,7 +102,7 @@
     return call(kernel, out, (weight, after), "HA", int(4e9), [pltpu.SemaphoreType.DMA((CHUNKS,))])
 
 
-def prepare(flags, image_slots, image_cot, text_rows, text_cot, destination, capacity):
+def prepare(image_slots, image_cot, text_rows, text_cot, destination, capacity):
     slots, feat = image_slots.shape
     two = slots == 2 * capacity
     text_dev = text_rows.shape[0]
@@ -111,12 +111,13 @@
     width = 2 * kept if two else kept
 
     def kernel(
-        flags_ref, slots_ref, cot_ref, text_ref, text_cot_ref, target_hbm,
+        slots_ref, cot_ref, text_ref, text_cot_ref, target_hbm,
         own_ref, give_ref, text_out_ref, select_ref, bits_ref, target_ref, sems,
     ):
+        group = lax.axis_index("group")
         pairs = [(target_hbm, target_ref)]
         for at, image, text in ((pl.ds(0, feat), slots_ref, text_ref), (pl.ds(feat, feat), cot_ref, text_cot_ref)):
-            start = flags_ref[0] * capacity if two else 0
+            start = group * capacity if two else 0
             pairs.append((image.at[pl.ds(start, kept)], own_ref.at[:, at]))
             pairs.append((text, text_out_ref.at[:, at]))
             if two:
@@ -125,13 +126,13 @@
         for copy in copies:
             copy.start()
         row = lax.broadcasted_iota(jnp.int32, bits_ref.shape, 0)
-        index = jnp.full(bits_ref.shape, flags_ref[1], jnp.int32)
+        index = jnp.full(bits_ref.shape, lax.axis_index("dp"), jnp.int32)
         bits_ref[...] = lax.shift_right_logical(index, row) & 1
         if not two:
             give_ref[...] = jnp.zeros_like(give_ref)
         copies[0].wait()
         target = [target_ref[i] for i in range(rows)]
-        first = flags_ref[0] if two else 0
+        first = group if two else 0
         position = lax.broadcasted_iota(jnp.int32, (rows, width), 0)
         lane = lax.broadcasted_iota(jnp.int32, (rows, width), 1)
         column = jnp.zeros((rows, width), jnp.int32)
@@ -153,9 +154,9 @@
         array((rows, width), F32),
         array((8, 128), jnp.int32),
     )
-    values = (flags, image_slots, image_cot, text_rows, text_cot, destination)
+    values = (image_slots, image_cot, text_rows, text_cot, destination)
     scratch = [pltpu.SMEM((rows,), jnp.int32), pltpu.SemaphoreType.DMA((7,))]
-    return call(kernel, out, values, "SHHHHH", 0, scratch)
+    return call(kernel, out, values, "HHHHH", 0, scratch)
 
 
 def pick(select, own, got, text, two):
@@ -224,9 +225,10 @@
 
 def forward_back(x, weight, after, parts, first, width):
     rows = x.shape[0]
-    step = 512 if width % 512 == 0 else 128
+    streamed = weight.shape[0] != width
+    step = 512 if streamed else 256
+    step = step if width % step == 0 else 128
     count = width // step
-    streamed = weight.shape[0] != width
 
     def kernel(x_ref, w_ref, after_ref, keep_ref, give_ref, *scratch):
         copies = []
@@ -239,7 +241,10 @@
             at = pl.ds(j * step, step)
             if streamed:
                 copies[j].wait()
-            out = lax.dot_general(x_ref[...], w_ref[at, :], NT, preferred_element_type=F32)
+            if streamed:
+                out = lax.dot_general(x_ref[...], w_ref[at, :], NT, preferred_element_type=F32)
+            else:
+                out = lax.dot_general(w_ref[at, :], x_ref[...], NT, preferred_element_type=F32).T
             split_store(out, keep_ref, give_ref, at, rows // parts)
 
     out = (array((rows // 2, width), F32), array((rows // 2, width), BF16))
@@ -279,21 +284,30 @@
     return pieces
 
 
-def backward(x, weight, added=None):
+def backward(x, weights, added=None):
     rows = x.shape[0]
-    feat = weight.shape[0]
-    step = 512 if feat % 512 == 0 else 128
+    feat = weights[0].shape[0]
+    step = 256
+    count = len(weights)
     more = 0 if added is None else 1
 
-    def kernel(x_ref, w_ref, *refs):
-        out_ref = refs[more]
+    def kernel(x_ref, *refs):
+        out_ref = refs[count + more]
         for j in range(feat // step):
             at = pl.ds(j * step, step)
-            out = lax.dot_general(x_ref[...], w_ref[at, :], NT, preferred_element_type=F32)
-            out_ref[:, at] = out + refs[0][:, at] if more else out
-
-    values = (x, in_vmem(weight), *([added] * more))
-    return call(kernel, array((rows, feat), F32), values, "VV" + "V" * more, 2 * rows * weight.size)
+            start = 0
+            out = None
+            for w_ref in refs[:count]:
+                columns = pl.ds(start, w_ref.shape[1])
+                term = lax.dot_general(w_ref[at, :], x_ref[:, columns], NT, preferred_element_type=F32)
+                out = term if out is None else out + term
+                start += w_ref.shape[1]
+            out = out.T
+            out_ref[:, at] = out + refs[count][:, at] if more else out
+
+    values = (x, *[in_vmem(w) for w in weights], *([added] * more))
+    flops = 2 * rows * feat * x.shape[1]
+    return call(kernel, array((rows, feat), F32), values, "V" * len(values), flops)
 
 
 def per_device(
@@ -305,9 +319,8 @@
     image_dev = destination.shape[0]
     feat, hidden = w_gate.shape
     two = groups == 2
-    flags = jnp.stack([lax.axis_index("group"), lax.axis_index("dp")]).astype(jnp.int32)
     target = destination.reshape(image_dev)
-    own, give, text, select, bits = prepare(flags, image_slots, image_cot, text_rows, text_cot, target, capacity)
+    own, give, text, select, bits = prepare(image_slots, image_cot, text_rows, text_cot, target, capacity)
     if two:
         got = swapped(give, "group", 1)
     else:
@@ -328,10 +341,12 @@
     keep_low, give_low = forward_back(cot, down_low, give, parts, 0, low)
     keep_high, give_high = forward_back(cot, w_down, sent, parts, low, hidden - low)
     both = halve_rest(both, "dp", sent)
-    keep = jnp.concatenate([keep_low, keep_high], axis=1)
-    give = jnp.concatenate([give_low, give_high], axis=1)
-    back = halve_first(give, keep, "dp")
-    back = halve_rest(back, "dp", sent_rows(back))
+    back_low = halve_first(give_low, keep_low, "dp")
+    back_high = halve_first(give_high, keep_high, "dp")
+    back_low = halve_rest(back_low, "dp", sent_rows(back_low))
+    sent = sent_rows(back_high)
+    back_high = halve_rest(back_high, "dp", sent)
+    back = jnp.concatenate([back_low, back_high], axis=1)
 
     gate = both[:, :hidden]
     up = both[:, hidden:]
@@ -340,8 +355,8 @@
     dup = (back * gate * sigmoid_gate).astype(BF16)
     spread_gate = by_xor(double(dgate, "dp"), bits)
     spread_up = by_xor(double(dup, "dp"), bits)
-    terms = backward(jnp.concatenate(spread_gate, axis=0), w_gate)
-    terms = backward(jnp.concatenate(spread_up, axis=0), w_up, terms)
+    terms = backward(jnp.concatenate(spread_gate, axis=0), (w_gate,))
+    terms = backward(jnp.concatenate(spread_up, axis=0), (w_up,), terms)
     grads = scatter_rows(blocks_of(terms, len(gathered)), "tp")
     image_grad = grads[:image_dev].astype(BF16)
     text_part = grads[image_dev:].astype(BF16)

time: 73.7 us -> 75.9 us (1.030)
  starting transfers between devices: 17.1 us -> 20.1 us
  Pallas kernels: 32.4 us -> 30.6 us
  waiting for transfers between devices: 19.1 us -> 20.2 us
    ppermute x15 -> x17, starting transfers between devices: 17.1 us -> 20.1 us  [swapped(): return lax.ppermute(value, axis, [(i, i ^ bit) for i in range(size)])]
    pallas_call x9, Pallas kernels: 32.4 us -> 30.6 us  [call(): pl.pallas_call(kernel, out_shape=out_shape, in_specs=[pl.BlockSpec(memory...]
    ppermute x15 -> x17, waiting for transfers between devices: 19.1 us -> 20.2 us  [swapped(): return lax.ppermute(value, axis, [(i, i ^ bit) for i in range(size)])]
  transfers between devices with their start and end apart: 15 -> 17, of which waited for: 10 -> 8; matrix products, arithmetic and copies ran while one was open for 1% -> 1% of each run, Pallas kernels for 27% -> 25%
where the time goes in v4:
time: 75.9 us; the launch traced here: 75.7 us
  Pallas kernels  30.6 us (40%)
  waiting for transfers between devices  20.2 us (27%)
  starting transfers between devices  20.1 us (26%)
  between operations  2.8 us (4%)
  other arithmetic  1.37 us (2%)
    pallas_call x9, Pallas kernels, call(): pl.pallas_call(kernel, out_shape=out_shape, in_specs=[pl.BlockSpec(memory...  30.6 us
    ppermute x17, waiting for transfers between devices, swapped(): return lax.ppermute(value, axis, [(i, i ^ bit) for i in range(size)])  20.2 us
    ppermute x17, starting transfers between devices, swapped(): return lax.ppermute(value, axis, [(i, i ^ bit) for i in range(size)])  20.1 us
  transfers between devices with their start and end apart: 17, of which 8 were waited for; matrix products, arithmetic and copies ran while one was open for 1% of the time, Pallas kernels for 25%

profile of v4, /device:TPU:0, one launch (start us, length us, event | category | flops | bytes accessed | tf_op | source)
XLA Modules:
  0.0 75.7 jit_solution(18333640155145979827)
XLA Ops:
  0.6 0.9 %shard_map.104 = (bf16[8,4096]{1,0:T(8,128)(2,1)S(1)}, bf16[8,4096]{1,0:T(8,128)(2,1)S(1)}, bf16[8,4096]{1,0:T(8,128)(2,1)S(1)}, f32[8,16]{1,0:T(8,128)S(1)}, s32[8,128]{1,0:T(8,128)S(1)}) custom-call(bf16[16,2048]{1,0:T(8,128)(2,1)} %slots_ref.1, bf16[16,2048]{1,0:T(8,128)(2,1)} %cot_ref.1, bf16[8,2048]{1,0:T(8,128)(2,1)} %text_ref.1, ...), custom_call_target="tpu_custom_call" | custom-call | flops 196640 | bytes 196640 | tf_op jit(solution)/shard_map/pallas_call | solution.py:33
  1.6 3.0 %collective-permute-start = (bf16[8,4096]{1,0:T(8,128)(2,1)S(1)}, bf16[8,4096]{1,0:T(8,128)(2,1)S(1)}, u32[]{:S(2)}, u32[]{:S(2)}) collective-permute-start(bf16[8,4096]{1,0:T(8,128)(2,1)S(1)} %get-tuple-element.17), channel_id=1, source_target_pairs={{0,16},{16,0},{1,17},{17,1},{2,18},{18,2},{3,19},{19,3},{4,20},{20... | collective-permute-start | bytes 196616 | tf_op jit(solution)/shard_map/ppermute | solution.py:46
  7.1 4.2 %collective-permute-start.1 = (bf16[16,4096]{1,0:T(8,128)(2,1)S(1)}, bf16[16,4096]{1,0:T(8,128)(2,1)S(1)}, u32[]{:S(2)}, u32[]{:S(2)}) collective-permute-start(bf16[16,4096]{1,0:T(8,128)(2,1)S(1)} %shard_map.105.after_ref), channel_id=1, source_target_pairs={{0,12},{4,8},{8,4},{12,0},{1,13},{5,9},{9,5},{13,1},{2,14},{6,10},... | collective-permute-start | bytes 393224 | tf_op jit(solution)/shard_map/ppermute | solution.py:46
  11.9 5.3 %shard_map.107.gate_ref.refs_0_ = bf16[2048,3584]{1,0:T(8,128)(2,1)S(1)} custom-call(bf16[2048,3584]{1,0:T(8,128)(2,1)} %w_ref.4, bf16[16,4096]{1,0:T(8,128)(2,1)S(1)} %shard_map.105.after_ref), custom_call_target="tpu_custom_call" | custom-call | flops 4000000000 | bytes 14811136 | tf_op jit(solution)/shard_map/pallas_call | solution.py:33
  17.2 4.0 %collective-permute-done.2 = bf16[16,4096]{1,0:T(8,128)(2,1)S(1)} collective-permute-done((bf16[16,4096]{1,0:T(8,128)(2,1)S(1)}, bf16[16,4096]{1,0:T(8,128)(2,1)S(1)}, u32[]{:S(2)}, u32[]{:S(2)}) %collective-permute-start.2) | collective-permute-done | bytes 131104 | tf_op jit(solution)/shard_map/ppermute | solution.py:46
  21.4 6.4 %shard_map.108 = (f32[32,7168]{1,0:T(8,128)S(1)}, bf16[32,7168]{1,0:T(8,128)(2,1)S(1)}, bf16[2048,3584]{1,0:T(8,128)(2,1)S(1)}) custom-call(bf16[64,2048]{1,0:T(8,128)(2,1)S(1)} %get-tuple-element.29.x_ref, bf16[2048,3584]{1,0:T(8,128)(2,1)S(1)} %shard_map.107.gate_ref.refs_0_, bf16[2048,3584]{1,0:T(8,128)(2,1)} %up_hbm.1), custom_call_target="tpu_custom_call" | custom-call | flops 1879048192 | bytes 29622272 | tf_op jit(solution)/shard_map/pallas_call | solution.py:33
  27.8 3.5 %shard_map.106.w_ref = bf16[2048,2048]{1,0:T(8,128)(2,1)S(1)} custom-call(bf16[3584,2048]{1,0:T(8,128)(2,1)} %w_ref.5, bf16[16,4096]{1,0:T(8,128)(2,1)S(1)} %shard_map.105.after_ref), custom_call_target="tpu_custom_call" | custom-call | flops 4000000000 | bytes 14811136 | tf_op jit(solution)/shard_map/pallas_call | solution.py:33
  31.3 2.4 %shard_map.109 = (f32[32,2048]{1,0:T(8,128)S(1)}, bf16[32,2048]{1,0:T(8,128)(2,1)S(1)}) custom-call(bf16[64,2048]{1,0:T(8,128)(2,1)S(1)} %get-tuple-element.28.x_ref, bf16[2048,2048]{1,0:T(8,128)(2,1)S(1)} %shard_map.106.w_ref, bf16[32,7168]{1,0:T(8,128)(2,1)S(1)} %get-tuple-element.19.after_ref), custom_call_target="tpu_custom_call" | custom-call | flops 536870912 | bytes 9109504 | tf_op jit(solution)/shard_map/pallas_call | solution.py:33
  34.3 3.9 %shard_map.110 = (f32[32,1536]{1,0:T(8,128)S(1)}, bf16[32,1536]{1,0:T(8,128)(2,1)S(1)}) custom-call(bf16[64,2048]{1,0:T(8,128)(2,1)S(1)} %get-tuple-element.28.x_ref, bf16[3584,2048]{1,0:T(8,128)(2,1)} %w_ref.5, bf16[16,7168]{1,0:T(8,128)(2,1)S(1)} %add_convert_fusion.after_ref), custom_call_target="tpu_custom_call" | custom-call | flops 402653184 | bytes 15171584 | tf_op jit(solution)/shard_map/pallas_call | solution.py:33
  38.4 1.6 %collective-permute-start.5 = (bf16[16,2048]{1,0:T(8,128)(2,1)S(1)}, bf16[16,2048]{1,0:T(8,128)(2,1)S(1)}, u32[]{:S(2)}, u32[]{:S(2)}) collective-permute-start(bf16[16,2048]{1,0:T(8,128)(2,1)S(1)} %add_convert_fusion.1), channel_id=1, source_target_pairs={{0,2},{1,3},{2,0},{3,1},{4,6},{5,7},{6,4},{7,5},{8,10},{9,11},{10,... | collective-permute-start | bytes 196616 | tf_op jit(solution)/shard_map/ppermute | solution.py:46
  40.0 1.2 %collective-permute-start.8 = (bf16[16,1536]{1,0:T(8,128)(2,1)S(1)}, bf16[16,1536]{1,0:T(8,128)(2,1)S(1)}, u32[]{:S(2)}, u32[]{:S(2)}) collective-permute-start(bf16[16,1536]{1,0:T(8,128)(2,1)S(1)} %add_convert_fusion.2), channel_id=1, source_target_pairs={{0,2},{1,3},{2,0},{3,1},{4,6},{5,7},{6,4},{7,5},{8,10},{9,11},{10,... | collective-permute-start | bytes 147464 | tf_op jit(solution)/shard_map/ppermute | solution.py:46
  41.2 1.8 %collective-permute-done.5 = bf16[16,2048]{1,0:T(8,128)(2,1)S(1)} collective-permute-done((bf16[16,2048]{1,0:T(8,128)(2,1)S(1)}, bf16[16,2048]{1,0:T(8,128)(2,1)S(1)}, u32[]{:S(2)}, u32[]{:S(2)}) %collective-permute-start.5) | collective-permute-done | bytes 65568 | tf_op jit(solution)/shard_map/ppermute | solution.py:46
  43.0 2.0 %collective-permute-start.9 = (bf16[16,7168]{1,0:T(8,128)(2,1)S(1)}, bf16[16,7168]{1,0:T(8,128)(2,1)S(1)}, u32[]{:S(2)}, u32[]{:S(2)}) collective-permute-start(bf16[16,7168]{1,0:T(8,128)(2,1)S(1)} %add_convert_fusion.after_ref), channel_id=1, source_target_pairs={{0,2},{1,3},{2,0},{3,1},{4,6},{5,7},{6,4},{7,5},{8,10},{9,11},{10,... | collective-permute-start | bytes 688136 | tf_op jit(solution)/shard_map/ppermute | solution.py:46
  45.0 5.1 %collective-permute-done.9 = bf16[16,7168]{1,0:T(8,128)(2,1)S(1)} collective-permute-done((bf16[16,7168]{1,0:T(8,128)(2,1)S(1)}, bf16[16,7168]{1,0:T(8,128)(2,1)S(1)}, u32[]{:S(2)}, u32[]{:S(2)}) %collective-permute-start.9) | collective-permute-done | bytes 229408 | tf_op jit(solution)/shard_map/ppermute | solution.py:46
  50.3 1.6 %collective-permute-start.12 = (bf16[16,3584]{1,0:T(8,128)(2,1)S(1)}, bf16[16,3584]{1,0:T(8,128)(2,1)S(1)}, u32[]{:S(2)}, u32[]{:S(2)}) collective-permute-start(bf16[16,3584]{1,0:T(8,128)(2,1)S(1)} %get-tuple-element.26), channel_id=1, source_target_pairs={{0,2},{1,3},{2,0},{3,1},{4,6},{5,7},{6,4},{7,5},{8,10},{9,11},{10,... | collective-permute-start | bytes 344072 | tf_op jit(solution)/shard_map/ppermute | solution.py:46
  53.2 2.5 %collective-permute-done.12 = bf16[16,3584]{1,0:T(8,128)(2,1)S(1)} collective-permute-done((bf16[16,3584]{1,0:T(8,128)(2,1)S(1)}, bf16[16,3584]{1,0:T(8,128)(2,1)S(1)}, u32[]{:S(2)}, u32[]{:S(2)}) %collective-permute-start.12) | collective-permute-done | bytes 114720 | tf_op jit(solution)/shard_map/ppermute | solution.py:46
  55.8 1.6 %collective-permute-done.10 = bf16[16,3584]{1,0:T(8,128)(2,1)S(1)} collective-permute-done((bf16[16,3584]{1,0:T(8,128)(2,1)S(1)}, bf16[16,3584]{1,0:T(8,128)(2,1)S(1)}, u32[]{:S(2)}, u32[]{:S(2)}) %collective-permute-start.10) | collective-permute-done | bytes 114720 | tf_op jit(solution)/shard_map/ppermute | solution.py:46
  57.6 4.0 %shard_map.111.refs_1_ = f32[64,2048]{1,0:T(8,128)S(1)} custom-call(bf16[64,3584]{1,0:T(8,128)(2,1)S(1)} %pad_maximum_fusion.2.x_ref, bf16[2048,3584]{1,0:T(8,128)(2,1)S(1)} %shard_map.107.gate_ref.refs_0_), custom_call_target="tpu_custom_call" | custom-call | flops 939524096 | bytes 15138816 | tf_op jit(solution)/shard_map/pallas_call | solution.py:33
  61.7 4.0 %shard_map.112 = f32[64,2048]{1,0:T(8,128)S(1)} custom-call(bf16[64,3584]{1,0:T(8,128)(2,1)S(1)} %pad_maximum_fusion.1.x_ref, bf16[2048,3584]{1,0:T(8,128)(2,1)S(1)} %get-tuple-element.25.refs_0_, f32[64,2048]{1,0:T(8,128)S(1)} %shard_map.111.refs_1_), custom_call_target="tpu_custom_call" | custom-call | flops 939524096 | bytes 15663104 | tf_op jit(solution)/shard_map/pallas_call | solution.py:33
  65.8 2.6 %collective-permute-start.16 = (bf16[16,2048]{1,0:T(8,128)(2,1)S(1)}, bf16[16,2048]{1,0:T(8,128)(2,1)S(1)}, u32[]{:S(2)}, u32[]{:S(2)}) collective-permute-start(bf16[16,2048]{1,0:T(8,128)(2,1)S(1)} %get-tuple-element.43), channel_id=1, source_target_pairs={{0,12},{4,8},{8,4},{12,0},{1,13},{5,9},{9,5},{13,1},{2,14},{6,10},... | collective-permute-start | bytes 196616 | tf_op jit(solution)/shard_map/ppermute | solution.py:46
  68.4 1.9 %collective-permute-start.14 = (bf16[16,2048]{1,0:T(8,128)(2,1)S(1)}, bf16[16,2048]{1,0:T(8,128)(2,1)S(1)}, u32[]{:S(2)}, u32[]{:S(2)}) collective-permute-start(bf16[16,2048]{1,0:T(8,128)(2,1)S(1)} %get-tuple-element.42), channel_id=1, source_target_pairs={{0,4},{4,0},{8,12},{12,8},{1,5},{5,1},{9,13},{13,9},{2,6},{6,2},{1... | collective-permute-start | bytes 196616 | tf_op jit(solution)/shard_map/ppermute | solution.py:46
  70.3 2.4 %collective-permute-done.16 = bf16[16,2048]{1,0:T(8,128)(2,1)S(1)} collective-permute-done((bf16[16,2048]{1,0:T(8,128)(2,1)S(1)}, bf16[16,2048]{1,0:T(8,128)(2,1)S(1)}, u32[]{:S(2)}, u32[]{:S(2)}) %collective-permute-start.16) | collective-permute-done | bytes 65568 | tf_op jit(solution)/shard_map/ppermute | solution.py:46
  72.7 2.3 %collective-permute-done.15 = bf16[16,2048]{1,0:T(8,128)(2,1)S(1)} collective-permute-done((bf16[16,2048]{1,0:T(8,128)(2,1)S(1)}, bf16[16,2048]{1,0:T(8,128)(2,1)S(1)}, u32[]{:S(2)}, u32[]{:S(2)}) %collective-permute-start.15) | collective-permute-done | bytes 65568 | tf_op jit(solution)/shard_map/ppermute | solution.py:46
  75.0 0.7 slice_select_fusion
  (41 shorter events, 4.0 us)
Async XLA Ops:
  1.6 5.3 %collective-permute-start = (bf16[8,4096]{1,0:T(8,128)(2,1)S(1)}, bf16[8,4096]{1,0:T(8,128)(2,1)S(1)}, u32[]{:S(2)}, u32[]{:S(2)}) collective-permute-start(bf16[8,4096]{1,0:T(8,128)(2,1)S(1)} %get-tuple-element.17), channel_id=1, source_target_pairs={{0,16},{16,0},{1,17},{17,1},{2,18},{18,2},{3,19},{19,3},{4,20},{20... | collective-permute-start | bytes 196616 | tf_op jit(solution)/shard_map/ppermute | solution.py:46
  7.1 10.1 %collective-permute-start.1 = (bf16[16,4096]{1,0:T(8,128)(2,1)S(1)}, bf16[16,4096]{1,0:T(8,128)(2,1)S(1)}, u32[]{:S(2)}, u32[]{:S(2)}) collective-permute-start(bf16[16,4096]{1,0:T(8,128)(2,1)S(1)} %shard_map.105.after_ref), channel_id=1, source_target_pairs={{0,12},{4,8},{8,4},{12,0},{1,13},{5,9},{9,5},{13,1},{2,14},{6,10},... | collective-permute-start | bytes 393224 | tf_op jit(solution)/shard_map/ppermute | solution.py:46
  11.3 9.9 %collective-permute-start.2 = (bf16[16,4096]{1,0:T(8,128)(2,1)S(1)}, bf16[16,4096]{1,0:T(8,128)(2,1)S(1)}, u32[]{:S(2)}, u32[]{:S(2)}) collective-permute-start(bf16[16,4096]{1,0:T(8,128)(2,1)S(1)} %shard_map.105.after_ref), channel_id=1, source_target_pairs={{0,8},{4,12},{8,0},{12,4},{1,9},{5,13},{9,1},{13,5},{2,10},{6,14},... | collective-permute-start | bytes 393224 | tf_op jit(solution)/shard_map/ppermute | solution.py:46
  11.3 9.9 %collective-permute-start.3 = (bf16[16,4096]{1,0:T(8,128)(2,1)S(1)}, bf16[16,4096]{1,0:T(8,128)(2,1)S(1)}, u32[]{:S(2)}, u32[]{:S(2)}) collective-permute-start(bf16[16,4096]{1,0:T(8,128)(2,1)S(1)} %shard_map.105.after_ref), channel_id=1, source_target_pairs={{0,4},{4,0},{8,12},{12,8},{1,5},{5,1},{9,13},{13,9},{2,6},{6,2},{1... | collective-permute-start | bytes 393224 | tf_op jit(solution)/shard_map/ppermute | solution.py:46
  27.7 6.6 %collective-permute-start.6 = (bf16[32,7168]{1,0:T(8,128)(2,1)S(1)}, bf16[32,7168]{1,0:T(8,128)(2,1)S(1)}, u32[]{:S(2)}, u32[]{:S(2)}) collective-permute-start(bf16[32,7168]{1,0:T(8,128)(2,1)S(1)} %get-tuple-element.19.after_ref), channel_id=1, source_target_pairs={{0,1},{1,0},{2,3},{3,2},{4,5},{5,4},{6,7},{7,6},{8,9},{9,8},{10,11... | collective-permute-start | bytes 1376264 | tf_op jit(solution)/shard_map/ppermute | solution.py:46
  33.7 4.6 %collective-permute-start.4 = (bf16[32,2048]{1,0:T(8,128)(2,1)S(1)}, bf16[32,2048]{1,0:T(8,128)(2,1)S(1)}, u32[]{:S(2)}, u32[]{:S(2)}) collective-permute-start(bf16[32,2048]{1,0:T(8,128)(2,1)S(1)} %get-tuple-element.21), channel_id=1, source_target_pairs={{0,1},{1,0},{2,3},{3,2},{4,5},{5,4},{6,7},{7,6},{8,9},{9,8},{10,11... | collective-permute-start | bytes 393224 | tf_op jit(solution)/shard_map/ppermute | solution.py:46
  38.2 1.7 %collective-permute-start.7 = (bf16[32,1536]{1,0:T(8,128)(2,1)S(1)}, bf16[32,1536]{1,0:T(8,128)(2,1)S(1)}, u32[]{:S(2)}, u32[]{:S(2)}) collective-permute-start(bf16[32,1536]{1,0:T(8,128)(2,1)S(1)} %get-tuple-element.24), channel_id=1, source_target_pairs={{0,1},{1,0},{2,3},{3,2},{4,5},{5,4},{6,7},{7,6},{8,9},{9,8},{10,11... | collective-permute-start | bytes 294920 | tf_op jit(solution)/shard_map/ppermute | solution.py:46
  38.4 4.6 %collective-permute-start.5 = (bf16[16,2048]{1,0:T(8,128)(2,1)S(1)}, bf16[16,2048]{1,0:T(8,128)(2,1)S(1)}, u32[]{:S(2)}, u32[]{:S(2)}) collective-permute-start(bf16[16,2048]{1,0:T(8,128)(2,1)S(1)} %add_convert_fusion.1), channel_id=1, source_target_pairs={{0,2},{1,3},{2,0},{3,1},{4,6},{5,7},{6,4},{7,5},{8,10},{9,11},{10,... | collective-permute-start | bytes 196616 | tf_op jit(solution)/shard_map/ppermute | solution.py:46
  40.0 5.0 %collective-permute-start.8 = (bf16[16,1536]{1,0:T(8,128)(2,1)S(1)}, bf16[16,1536]{1,0:T(8,128)(2,1)S(1)}, u32[]{:S(2)}, u32[]{:S(2)}) collective-permute-start(bf16[16,1536]{1,0:T(8,128)(2,1)S(1)} %add_convert_fusion.2), channel_id=1, source_target_pairs={{0,2},{1,3},{2,0},{3,1},{4,6},{5,7},{6,4},{7,5},{8,10},{9,11},{10,... | collective-permute-start | bytes 147464 | tf_op jit(solution)/shard_map/ppermute | solution.py:46
  43.0 7.1 %collective-permute-start.9 = (bf16[16,7168]{1,0:T(8,128)(2,1)S(1)}, bf16[16,7168]{1,0:T(8,128)(2,1)S(1)}, u32[]{:S(2)}, u32[]{:S(2)}) collective-permute-start(bf16[16,7168]{1,0:T(8,128)(2,1)S(1)} %add_convert_fusion.after_ref), channel_id=1, source_target_pairs={{0,2},{1,3},{2,0},{3,1},{4,6},{5,7},{6,4},{7,5},{8,10},{9,11},{10,... | collective-permute-start | bytes 688136 | tf_op jit(solution)/shard_map/ppermute | solution.py:46
  50.3 5.4 %collective-permute-start.12 = (bf16[16,3584]{1,0:T(8,128)(2,1)S(1)}, bf16[16,3584]{1,0:T(8,128)(2,1)S(1)}, u32[]{:S(2)}, u32[]{:S(2)}) collective-permute-start(bf16[16,3584]{1,0:T(8,128)(2,1)S(1)} %get-tuple-element.26), channel_id=1, source_target_pairs={{0,2},{1,3},{2,0},{3,1},{4,6},{5,7},{6,4},{7,5},{8,10},{9,11},{10,... | collective-permute-start | bytes 344072 | tf_op jit(solution)/shard_map/ppermute | solution.py:46
  52.6 4.9 %collective-permute-start.10 = (bf16[16,3584]{1,0:T(8,128)(2,1)S(1)}, bf16[16,3584]{1,0:T(8,128)(2,1)S(1)}, u32[]{:S(2)}, u32[]{:S(2)}) collective-permute-start(bf16[16,3584]{1,0:T(8,128)(2,1)S(1)} %get-tuple-element.27), channel_id=1, source_target_pairs={{0,2},{1,3},{2,0},{3,1},{4,6},{5,7},{6,4},{7,5},{8,10},{9,11},{10,... | collective-permute-start | bytes 344072 | tf_op jit(solution)/shard_map/ppermute | solution.py:46
  55.7 1.8 %collective-permute-start.13 = (bf16[32,3584]{1,0:T(8,128)(2,1)S(1)}, bf16[32,3584]{1,0:T(8,128)(2,1)S(1)}, u32[]{:S(2)}, u32[]{:S(2)}) collective-permute-start(bf16[32,3584]{1,0:T(8,128)(2,1)S(1)} %pad_maximum_fusion.5), channel_id=1, source_target_pairs={{0,1},{1,0},{2,3},{3,2},{4,5},{5,4},{6,7},{7,6},{8,9},{9,8},{10,11... | collective-permute-start | bytes 688136 | tf_op jit(solution)/shard_map/ppermute | solution.py:46
  57.4 4.2 %collective-permute-start.11 = (bf16[32,3584]{1,0:T(8,128)(2,1)S(1)}, bf16[32,3584]{1,0:T(8,128)(2,1)S(1)}, u32[]{:S(2)}, u32[]{:S(2)}) collective-permute-start(bf16[32,3584]{1,0:T(8,128)(2,1)S(1)} %pad_maximum_fusion.4), channel_id=1, source_target_pairs={{0,1},{1,0},{2,3},{3,2},{4,5},{5,4},{6,7},{7,6},{8,9},{9,8},{10,11... | collective-permute-start | bytes 688136 | tf_op jit(solution)/shard_map/ppermute | solution.py:46
  65.8 6.9 %collective-permute-start.16 = (bf16[16,2048]{1,0:T(8,128)(2,1)S(1)}, bf16[16,2048]{1,0:T(8,128)(2,1)S(1)}, u32[]{:S(2)}, u32[]{:S(2)}) collective-permute-start(bf16[16,2048]{1,0:T(8,128)(2,1)S(1)} %get-tuple-element.43), channel_id=1, source_target_pairs={{0,12},{4,8},{8,4},{12,0},{1,13},{5,9},{9,5},{13,1},{2,14},{6,10},... | collective-permute-start | bytes 196616 | tf_op jit(solution)/shard_map/ppermute | solution.py:46
  68.4 6.6 %collective-permute-start.15 = (bf16[16,2048]{1,0:T(8,128)(2,1)S(1)}, bf16[16,2048]{1,0:T(8,128)(2,1)S(1)}, u32[]{:S(2)}, u32[]{:S(2)}) collective-permute-start(bf16[16,2048]{1,0:T(8,128)(2,1)S(1)} %get-tuple-element.44), channel_id=1, source_target_pairs={{0,8},{4,12},{8,0},{12,4},{1,9},{5,13},{9,1},{13,5},{2,10},{6,14},... | collective-permute-start | bytes 196616 | tf_op jit(solution)/shard_map/ppermute | solution.py:46
  68.4 6.6 %collective-permute-start.14 = (bf16[16,2048]{1,0:T(8,128)(2,1)S(1)}, bf16[16,2048]{1,0:T(8,128)(2,1)S(1)}, u32[]{:S(2)}, u32[]{:S(2)}) collective-permute-start(bf16[16,2048]{1,0:T(8,128)(2,1)S(1)} %get-tuple-element.42), channel_id=1, source_target_pairs={{0,4},{4,0},{8,12},{12,8},{1,5},{5,1},{9,13},{13,9},{2,6},{6,2},{1... | collective-permute-start | bytes 196616 | tf_op jit(solution)/shard_map/ppermute | solution.py:46

commit v5 on v4

--- a/solution.py
+++ b/solution.py
@@ -223,39 +223,38 @@
     return call(kernel, out, values, "VVH", 4 * rows * w_up.size, scratch)
 
 
-def forward_back(x, weight, after, parts, first, width):
+def forward_back(x, low, weight, after, parts, first, width):
     rows = x.shape[0]
-    streamed = weight.shape[0] != width
-    step = 512 if streamed else 256
-    step = step if width % step == 0 else 128
-    count = width // step
-
-    def kernel(x_ref, w_ref, after_ref, keep_ref, give_ref, *scratch):
+    held = min(low.shape[0] - first, width)
+    rest = width - held
+    step = 512 if rest % 512 == 0 else 128
+    count = rest // step
+
+    def kernel(x_ref, low_ref, w_ref, after_ref, keep_ref, give_ref, *scratch):
         copies = []
-        if streamed:
-            copies = copies_of(w_ref.at[pl.ds(first, width)], *scratch, count)
-            w_ref = scratch[0]
+        if rest:
+            copies = copies_of(w_ref.at[pl.ds(first + held, rest)], *scratch, count)
         for copy in copies:
             copy.start()
-        for j in range(count):
+        size = 256 if held % 256 == 0 else 128
+        for j in range(held // size):
+            at = pl.ds(j * size, size)
+            out = lax.dot_general(low_ref[pl.ds(first + j * size, size), :], x_ref[...], NT, preferred_element_type=F32)
+            split_store(out.T, keep_ref, give_ref, at, rows // parts)
+        for j, copy in enumerate(copies):
+            copy.wait()
             at = pl.ds(j * step, step)
-            if streamed:
-                copies[j].wait()
-            if streamed:
-                out = lax.dot_general(x_ref[...], w_ref[at, :], NT, preferred_element_type=F32)
-            else:
-                out = lax.dot_general(w_ref[at, :], x_ref[...], NT, preferred_element_type=F32).T
-            split_store(out, keep_ref, give_ref, at, rows // parts)
+            out = lax.dot_general(x_ref[...], scratch[0][at, :], NT, preferred_element_type=F32)
+            split_store(out, keep_ref, give_ref, pl.ds(held + j * step, step), rows // parts)
 
     out = (array((rows // 2, width), F32), array((rows // 2, width), BF16))
     scratch = []
-    extra = 0
-    if streamed:
-        scratch = [pltpu.VMEM((width, weight.shape[1]), weight.dtype), pltpu.SemaphoreType.DMA((count,))]
-        extra = width * weight.shape[1] * 2
-    values = (x, weight if streamed else in_vmem(weight), after)
+    if rest:
+        scratch = [pltpu.VMEM((rest, weight.shape[1]), weight.dtype), pltpu.SemaphoreType.DMA((count,))]
+    values = (x, in_vmem(low), weight, after)
     flops = 2 * rows * width * weight.shape[1]
-    return call(kernel, out, values, "VHA" if streamed else "VVA", flops, scratch, extra)
+    extra = 2 * rest * weight.shape[1]
+    return call(kernel, out, values, "VVHA", flops, scratch, extra)
 
 
 def halve_first(give, keep, axis):
@@ -338,12 +337,14 @@
     both = halve_first(give, keep, "dp")
     cot = rows[:, feat:]
     sent = sent_rows(both)
-    keep_low, give_low = forward_back(cot, down_low, give, parts, 0, low)
-    keep_high, give_high = forward_back(cot, w_down, sent, parts, low, hidden - low)
+    split = max(low - 512, 256)
+    keep_low, give_low = forward_back(cot, down_low, w_down, give, parts, 0, split)
+    keep_high, give_high = forward_back(cot, down_low, w_down, sent, parts, split, hidden - split)
     both = halve_rest(both, "dp", sent)
     back_low = halve_first(give_low, keep_low, "dp")
     back_high = halve_first(give_high, keep_high, "dp")
-    back_low = halve_rest(back_low, "dp", sent_rows(back_low))
+    sent = sent_rows(back_low)
+    back_low = halve_rest(back_low, "dp", sent)
     sent = sent_rows(back_high)
     back_high = halve_rest(back_high, "dp", sent)
     back = jnp.concatenate([back_low, back_high], axis=1)

time: 75.9 us -> 75.1 us (0.989)
  transfers between devices with their start and end apart: 17 -> 17, of which waited for: 8 -> 10; matrix products, arithmetic and copies ran while one was open for 1% -> 1% of each run, Pallas kernels for 25% -> 25%
where the time goes in v5:
time: 75.1 us; the launch traced here: 74.8 us
  Pallas kernels  30.1 us (40%)
  waiting for transfers between devices  20.1 us (27%)
  starting transfers between devices  19.9 us (26%)
  between operations  2.81 us (4%)
  other arithmetic  1.36 us (2%)
    pallas_call x9, Pallas kernels, call(): pl.pallas_call(kernel, out_shape=out_shape, in_specs=[pl.BlockSpec(memory...  30.1 us
    ppermute x17, waiting for transfers between devices, swapped(): return lax.ppermute(value, axis, [(i, i ^ bit) for i in range(size)])  20.1 us
    ppermute x17, starting transfers between devices, swapped(): return lax.ppermute(value, axis, [(i, i ^ bit) for i in range(size)])  19.9 us
  transfers between devices with their start and end apart: 17, of which 10 were waited for; matrix products, arithmetic and copies ran while one was open for 1% of the time, Pallas kernels for 25%

profile of v5, /device:TPU:0, one launch (start us, length us, event | category | flops | bytes accessed | tf_op | source)
XLA Modules:
  0.0 74.8 jit_solution(3824349391337224548)
XLA Ops:
  0.6 0.9 %shard_map.104 = (bf16[8,4096]{1,0:T(8,128)(2,1)S(1)}, bf16[8,4096]{1,0:T(8,128)(2,1)S(1)}, bf16[8,4096]{1,0:T(8,128)(2,1)S(1)}, f32[8,16]{1,0:T(8,128)S(1)}, s32[8,128]{1,0:T(8,128)S(1)}) custom-call(bf16[16,2048]{1,0:T(8,128)(2,1)} %slots_ref.1, bf16[16,2048]{1,0:T(8,128)(2,1)} %cot_ref.1, bf16[8,2048]{1,0:T(8,128)(2,1)} %text_ref.1, ...), custom_call_target="tpu_custom_call" | custom-call | flops 196640 | bytes 196640 | tf_op jit(solution)/shard_map/pallas_call | solution.py:33
  1.6 3.0 %collective-permute-start = (bf16[8,4096]{1,0:T(8,128)(2,1)S(1)}, bf16[8,4096]{1,0:T(8,128)(2,1)S(1)}, u32[]{:S(2)}, u32[]{:S(2)}) collective-permute-start(bf16[8,4096]{1,0:T(8,128)(2,1)S(1)} %get-tuple-element.17), channel_id=1, source_target_pairs={{0,16},{16,0},{1,17},{17,1},{2,18},{18,2},{3,19},{19,3},{4,20},{20... | collective-permute-start | bytes 196616 | tf_op jit(solution)/shard_map/ppermute | solution.py:46
  7.1 4.2 %collective-permute-start.1 = (bf16[16,4096]{1,0:T(8,128)(2,1)S(1)}, bf16[16,4096]{1,0:T(8,128)(2,1)S(1)}, u32[]{:S(2)}, u32[]{:S(2)}) collective-permute-start(bf16[16,4096]{1,0:T(8,128)(2,1)S(1)} %shard_map.105.after_ref), channel_id=1, source_target_pairs={{0,12},{4,8},{8,4},{12,0},{1,13},{5,9},{9,5},{13,1},{2,14},{6,10},... | collective-permute-start | bytes 393224 | tf_op jit(solution)/shard_map/ppermute | solution.py:46
  11.9 5.3 %shard_map.107.gate_ref.refs_0_ = bf16[2048,3584]{1,0:T(8,128)(2,1)S(1)} custom-call(bf16[2048,3584]{1,0:T(8,128)(2,1)} %w_ref.5, bf16[16,4096]{1,0:T(8,128)(2,1)S(1)} %shard_map.105.after_ref), custom_call_target="tpu_custom_call" | custom-call | flops 4000000000 | bytes 14811136 | tf_op jit(solution)/shard_map/pallas_call | solution.py:33
  17.2 4.0 %collective-permute-done.2 = bf16[16,4096]{1,0:T(8,128)(2,1)S(1)} collective-permute-done((bf16[16,4096]{1,0:T(8,128)(2,1)S(1)}, bf16[16,4096]{1,0:T(8,128)(2,1)S(1)}, u32[]{:S(2)}, u32[]{:S(2)}) %collective-permute-start.2) | collective-permute-done | bytes 131104 | tf_op jit(solution)/shard_map/ppermute | solution.py:46
  21.4 6.4 %shard_map.108 = (f32[32,7168]{1,0:T(8,128)S(1)}, bf16[32,7168]{1,0:T(8,128)(2,1)S(1)}, bf16[2048,3584]{1,0:T(8,128)(2,1)S(1)}) custom-call(bf16[64,2048]{1,0:T(8,128)(2,1)S(1)} %get-tuple-element.29.x_ref, bf16[2048,3584]{1,0:T(8,128)(2,1)S(1)} %shard_map.107.gate_ref.refs_0_, bf16[2048,3584]{1,0:T(8,128)(2,1)} %up_hbm.1), custom_call_target="tpu_custom_call" | custom-call | flops 1879048192 | bytes 29622272 | tf_op jit(solution)/shard_map/pallas_call | solution.py:33
  27.8 3.5 %shard_map.106.low_ref = bf16[2048,2048]{1,0:T(8,128)(2,1)S(1)} custom-call(bf16[3584,2048]{1,0:T(8,128)(2,1)} %w_ref.7, bf16[16,4096]{1,0:T(8,128)(2,1)S(1)} %shard_map.105.after_ref), custom_call_target="tpu_custom_call" | custom-call | flops 4000000000 | bytes 14811136 | tf_op jit(solution)/shard_map/pallas_call | solution.py:33
  31.3 1.8 %shard_map.109 = (f32[32,1536]{1,0:T(8,128)S(1)}, bf16[32,1536]{1,0:T(8,128)(2,1)S(1)}) custom-call(bf16[64,2048]{1,0:T(8,128)(2,1)S(1)} %get-tuple-element.28.x_ref, bf16[2048,2048]{1,0:T(8,128)(2,1)S(1)} %shard_map.106.low_ref, bf16[3584,2048]{1,0:T(8,128)(2,1)} %w_ref.7, bf16[32,7168]{1,0:T(8,128)(2,1)S(1)} %get-tuple-element.19.after_ref), custom_call_target="tpu_custom_call" | custom-call | flops 402653184 | bytes 23789568 | tf_op jit(solution)/shard_map/pallas_call | solution.py:33
  33.8 3.9 %shard_map.110 = (f32[32,2048]{1,0:T(8,128)S(1)}, bf16[32,2048]{1,0:T(8,128)(2,1)S(1)}) custom-call(bf16[64,2048]{1,0:T(8,128)(2,1)S(1)} %get-tuple-element.28.x_ref, bf16[2048,2048]{1,0:T(8,128)(2,1)S(1)} %shard_map.106.low_ref, bf16[3584,2048]{1,0:T(8,128)(2,1)} %w_ref.7, bf16[16,7168]{1,0:T(8,128)(2,1)S(1)} %add_convert_fusion.after_ref), custom_call_target="tpu_custom_call" | custom-call | flops 536870912 | bytes 23560192 | tf_op jit(solution)/shard_map/pallas_call | solution.py:33
  37.8 1.6 %collective-permute-start.5 = (bf16[16,1536]{1,0:T(8,128)(2,1)S(1)}, bf16[16,1536]{1,0:T(8,128)(2,1)S(1)}, u32[]{:S(2)}, u32[]{:S(2)}) collective-permute-start(bf16[16,1536]{1,0:T(8,128)(2,1)S(1)} %add_convert_fusion.2), channel_id=1, source_target_pairs={{0,2},{1,3},{2,0},{3,1},{4,6},{5,7},{6,4},{7,5},{8,10},{9,11},{10,... | collective-permute-start | bytes 147464 | tf_op jit(solution)/shard_map/ppermute | solution.py:46
  39.4 1.3 %collective-permute-start.8 = (bf16[16,2048]{1,0:T(8,128)(2,1)S(1)}, bf16[16,2048]{1,0:T(8,128)(2,1)S(1)}, u32[]{:S(2)}, u32[]{:S(2)}) collective-permute-start(bf16[16,2048]{1,0:T(8,128)(2,1)S(1)} %add_convert_fusion.1), channel_id=1, source_target_pairs={{0,2},{1,3},{2,0},{3,1},{4,6},{5,7},{6,4},{7,5},{8,10},{9,11},{10,... | collective-permute-start | bytes 196616 | tf_op jit(solution)/shard_map/ppermute | solution.py:46
  40.7 1.3 %collective-permute-done.5 = bf16[16,1536]{1,0:T(8,128)(2,1)S(1)} collective-permute-done((bf16[16,1536]{1,0:T(8,128)(2,1)S(1)}, bf16[16,1536]{1,0:T(8,128)(2,1)S(1)}, u32[]{:S(2)}, u32[]{:S(2)}) %collective-permute-start.5) | collective-permute-done | bytes 49184 | tf_op jit(solution)/shard_map/ppermute | solution.py:46
  42.1 1.6 %collective-permute-start.9 = (bf16[16,7168]{1,0:T(8,128)(2,1)S(1)}, bf16[16,7168]{1,0:T(8,128)(2,1)S(1)}, u32[]{:S(2)}, u32[]{:S(2)}) collective-permute-start(bf16[16,7168]{1,0:T(8,128)(2,1)S(1)} %add_convert_fusion.after_ref), channel_id=1, source_target_pairs={{0,2},{1,3},{2,0},{3,1},{4,6},{5,7},{6,4},{7,5},{8,10},{9,11},{10,... | collective-permute-start | bytes 688136 | tf_op jit(solution)/shard_map/ppermute | solution.py:46
  43.8 5.5 %collective-permute-done.9 = bf16[16,7168]{1,0:T(8,128)(2,1)S(1)} collective-permute-done((bf16[16,7168]{1,0:T(8,128)(2,1)S(1)}, bf16[16,7168]{1,0:T(8,128)(2,1)S(1)}, u32[]{:S(2)}, u32[]{:S(2)}) %collective-permute-start.9) | collective-permute-done | bytes 229408 | tf_op jit(solution)/shard_map/ppermute | solution.py:46
  49.5 1.6 %collective-permute-start.12 = (bf16[16,3584]{1,0:T(8,128)(2,1)S(1)}, bf16[16,3584]{1,0:T(8,128)(2,1)S(1)}, u32[]{:S(2)}, u32[]{:S(2)}) collective-permute-start(bf16[16,3584]{1,0:T(8,128)(2,1)S(1)} %get-tuple-element.26), channel_id=1, source_target_pairs={{0,2},{1,3},{2,0},{3,1},{4,6},{5,7},{6,4},{7,5},{8,10},{9,11},{10,... | collective-permute-start | bytes 344072 | tf_op jit(solution)/shard_map/ppermute | solution.py:46
  52.3 3.0 %collective-permute-done.12 = bf16[16,3584]{1,0:T(8,128)(2,1)S(1)} collective-permute-done((bf16[16,3584]{1,0:T(8,128)(2,1)S(1)}, bf16[16,3584]{1,0:T(8,128)(2,1)S(1)}, u32[]{:S(2)}, u32[]{:S(2)}) %collective-permute-start.12) | collective-permute-done | bytes 114720 | tf_op jit(solution)/shard_map/ppermute | solution.py:46
  55.3 1.2 %collective-permute-done.10 = bf16[16,3584]{1,0:T(8,128)(2,1)S(1)} collective-permute-done((bf16[16,3584]{1,0:T(8,128)(2,1)S(1)}, bf16[16,3584]{1,0:T(8,128)(2,1)S(1)}, u32[]{:S(2)}, u32[]{:S(2)}) %collective-permute-start.10) | collective-permute-done | bytes 114720 | tf_op jit(solution)/shard_map/ppermute | solution.py:46
  56.9 4.0 %shard_map.111.refs_1_ = f32[64,2048]{1,0:T(8,128)S(1)} custom-call(bf16[64,3584]{1,0:T(8,128)(2,1)S(1)} %pad_maximum_fusion.2.x_ref, bf16[2048,3584]{1,0:T(8,128)(2,1)S(1)} %shard_map.107.gate_ref.refs_0_), custom_call_target="tpu_custom_call" | custom-call | flops 939524096 | bytes 15138816 | tf_op jit(solution)/shard_map/pallas_call | solution.py:33
  61.0 4.0 %shard_map.112 = f32[64,2048]{1,0:T(8,128)S(1)} custom-call(bf16[64,3584]{1,0:T(8,128)(2,1)S(1)} %pad_maximum_fusion.1.x_ref, bf16[2048,3584]{1,0:T(8,128)(2,1)S(1)} %get-tuple-element.25.refs_0_, f32[64,2048]{1,0:T(8,128)S(1)} %shard_map.111.refs_1_), custom_call_target="tpu_custom_call" | custom-call | flops 939524096 | bytes 15663104 | tf_op jit(solution)/shard_map/pallas_call | solution.py:33
  65.1 2.5 %collective-permute-start.16 = (bf16[16,2048]{1,0:T(8,128)(2,1)S(1)}, bf16[16,2048]{1,0:T(8,128)(2,1)S(1)}, u32[]{:S(2)}, u32[]{:S(2)}) collective-permute-start(bf16[16,2048]{1,0:T(8,128)(2,1)S(1)} %get-tuple-element.43), channel_id=1, source_target_pairs={{0,12},{4,8},{8,4},{12,0},{1,13},{5,9},{9,5},{13,1},{2,14},{6,10},... | collective-permute-start | bytes 196616 | tf_op jit(solution)/shard_map/ppermute | solution.py:46
  67.6 1.9 %collective-permute-start.14 = (bf16[16,2048]{1,0:T(8,128)(2,1)S(1)}, bf16[16,2048]{1,0:T(8,128)(2,1)S(1)}, u32[]{:S(2)}, u32[]{:S(2)}) collective-permute-start(bf16[16,2048]{1,0:T(8,128)(2,1)S(1)} %get-tuple-element.42), channel_id=1, source_target_pairs={{0,4},{4,0},{8,12},{12,8},{1,5},{5,1},{9,13},{13,9},{2,6},{6,2},{1... | collective-permute-start | bytes 196616 | tf_op jit(solution)/shard_map/ppermute | solution.py:46
  69.6 2.4 %collective-permute-done.16 = bf16[16,2048]{1,0:T(8,128)(2,1)S(1)} collective-permute-done((bf16[16,2048]{1,0:T(8,128)(2,1)S(1)}, bf16[16,2048]{1,0:T(8,128)(2,1)S(1)}, u32[]{:S(2)}, u32[]{:S(2)}) %collective-permute-start.16) | collective-permute-done | bytes 65568 | tf_op jit(solution)/shard_map/ppermute | solution.py:46
  72.0 2.1 %collective-permute-done.15 = bf16[16,2048]{1,0:T(8,128)(2,1)S(1)} collective-permute-done((bf16[16,2048]{1,0:T(8,128)(2,1)S(1)}, bf16[16,2048]{1,0:T(8,128)(2,1)S(1)}, u32[]{:S(2)}, u32[]{:S(2)}) %collective-permute-start.15) | collective-permute-done | bytes 65568 | tf_op jit(solution)/shard_map/ppermute | solution.py:46
  74.2 0.7 slice_select_fusion
  (41 shorter events, 4.2 us)
Async XLA Ops:
  1.6 5.3 %collective-permute-start = (bf16[8,4096]{1,0:T(8,128)(2,1)S(1)}, bf16[8,4096]{1,0:T(8,128)(2,1)S(1)}, u32[]{:S(2)}, u32[]{:S(2)}) collective-permute-start(bf16[8,4096]{1,0:T(8,128)(2,1)S(1)} %get-tuple-element.17), channel_id=1, source_target_pairs={{0,16},{16,0},{1,17},{17,1},{2,18},{18,2},{3,19},{19,3},{4,20},{20... | collective-permute-start | bytes 196616 | tf_op jit(solution)/shard_map/ppermute | solution.py:46
  7.1 10.1 %collective-permute-start.1 = (bf16[16,4096]{1,0:T(8,128)(2,1)S(1)}, bf16[16,4096]{1,0:T(8,128)(2,1)S(1)}, u32[]{:S(2)}, u32[]{:S(2)}) collective-permute-start(bf16[16,4096]{1,0:T(8,128)(2,1)S(1)} %shard_map.105.after_ref), channel_id=1, source_target_pairs={{0,12},{4,8},{8,4},{12,0},{1,13},{5,9},{9,5},{13,1},{2,14},{6,10},... | collective-permute-start | bytes 393224 | tf_op jit(solution)/shard_map/ppermute | solution.py:46
  11.3 9.9 %collective-permute-start.2 = (bf16[16,4096]{1,0:T(8,128)(2,1)S(1)}, bf16[16,4096]{1,0:T(8,128)(2,1)S(1)}, u32[]{:S(2)}, u32[]{:S(2)}) collective-permute-start(bf16[16,4096]{1,0:T(8,128)(2,1)S(1)} %shard_map.105.after_ref), channel_id=1, source_target_pairs={{0,8},{4,12},{8,0},{12,4},{1,9},{5,13},{9,1},{13,5},{2,10},{6,14},... | collective-permute-start | bytes 393224 | tf_op jit(solution)/shard_map/ppermute | solution.py:46
  11.3 9.9 %collective-permute-start.3 = (bf16[16,4096]{1,0:T(8,128)(2,1)S(1)}, bf16[16,4096]{1,0:T(8,128)(2,1)S(1)}, u32[]{:S(2)}, u32[]{:S(2)}) collective-permute-start(bf16[16,4096]{1,0:T(8,128)(2,1)S(1)} %shard_map.105.after_ref), channel_id=1, source_target_pairs={{0,4},{4,0},{8,12},{12,8},{1,5},{5,1},{9,13},{13,9},{2,6},{6,2},{1... | collective-permute-start | bytes 393224 | tf_op jit(solution)/shard_map/ppermute | solution.py:46
  27.8 6.0 %collective-permute-start.6 = (bf16[32,7168]{1,0:T(8,128)(2,1)S(1)}, bf16[32,7168]{1,0:T(8,128)(2,1)S(1)}, u32[]{:S(2)}, u32[]{:S(2)}) collective-permute-start(bf16[32,7168]{1,0:T(8,128)(2,1)S(1)} %get-tuple-element.19.after_ref), channel_id=1, source_target_pairs={{0,1},{1,0},{2,3},{3,2},{4,5},{5,4},{6,7},{7,6},{8,9},{9,8},{10,11... | collective-permute-start | bytes 1376264 | tf_op jit(solution)/shard_map/ppermute | solution.py:46
  33.2 4.6 %collective-permute-start.4 = (bf16[32,1536]{1,0:T(8,128)(2,1)S(1)}, bf16[32,1536]{1,0:T(8,128)(2,1)S(1)}, u32[]{:S(2)}, u32[]{:S(2)}) collective-permute-start(bf16[32,1536]{1,0:T(8,128)(2,1)S(1)} %get-tuple-element.21), channel_id=1, source_target_pairs={{0,1},{1,0},{2,3},{3,2},{4,5},{5,4},{6,7},{7,6},{8,9},{9,8},{10,11... | collective-permute-start | bytes 294920 | tf_op jit(solution)/shard_map/ppermute | solution.py:46
  37.7 1.7 %collective-permute-start.7 = (bf16[32,2048]{1,0:T(8,128)(2,1)S(1)}, bf16[32,2048]{1,0:T(8,128)(2,1)S(1)}, u32[]{:S(2)}, u32[]{:S(2)}) collective-permute-start(bf16[32,2048]{1,0:T(8,128)(2,1)S(1)} %get-tuple-element.24), channel_id=1, source_target_pairs={{0,1},{1,0},{2,3},{3,2},{4,5},{5,4},{6,7},{7,6},{8,9},{9,8},{10,11... | collective-permute-start | bytes 393224 | tf_op jit(solution)/shard_map/ppermute | solution.py:46
  37.8 4.2 %collective-permute-start.5 = (bf16[16,1536]{1,0:T(8,128)(2,1)S(1)}, bf16[16,1536]{1,0:T(8,128)(2,1)S(1)}, u32[]{:S(2)}, u32[]{:S(2)}) collective-permute-start(bf16[16,1536]{1,0:T(8,128)(2,1)S(1)} %add_convert_fusion.2), channel_id=1, source_target_pairs={{0,2},{1,3},{2,0},{3,1},{4,6},{5,7},{6,4},{7,5},{8,10},{9,11},{10,... | collective-permute-start | bytes 147464 | tf_op jit(solution)/shard_map/ppermute | solution.py:46
  39.4 4.3 %collective-permute-start.8 = (bf16[16,2048]{1,0:T(8,128)(2,1)S(1)}, bf16[16,2048]{1,0:T(8,128)(2,1)S(1)}, u32[]{:S(2)}, u32[]{:S(2)}) collective-permute-start(bf16[16,2048]{1,0:T(8,128)(2,1)S(1)} %add_convert_fusion.1), channel_id=1, source_target_pairs={{0,2},{1,3},{2,0},{3,1},{4,6},{5,7},{6,4},{7,5},{8,10},{9,11},{10,... | collective-permute-start | bytes 196616 | tf_op jit(solution)/shard_map/ppermute | solution.py:46
  42.1 7.2 %collective-permute-start.9 = (bf16[16,7168]{1,0:T(8,128)(2,1)S(1)}, bf16[16,7168]{1,0:T(8,128)(2,1)S(1)}, u32[]{:S(2)}, u32[]{:S(2)}) collective-permute-start(bf16[16,7168]{1,0:T(8,128)(2,1)S(1)} %add_convert_fusion.after_ref), channel_id=1, source_target_pairs={{0,2},{1,3},{2,0},{3,1},{4,6},{5,7},{6,4},{7,5},{8,10},{9,11},{10,... | collective-permute-start | bytes 688136 | tf_op jit(solution)/shard_map/ppermute | solution.py:46
  49.5 5.8 %collective-permute-start.12 = (bf16[16,3584]{1,0:T(8,128)(2,1)S(1)}, bf16[16,3584]{1,0:T(8,128)(2,1)S(1)}, u32[]{:S(2)}, u32[]{:S(2)}) collective-permute-start(bf16[16,3584]{1,0:T(8,128)(2,1)S(1)} %get-tuple-element.26), channel_id=1, source_target_pairs={{0,2},{1,3},{2,0},{3,1},{4,6},{5,7},{6,4},{7,5},{8,10},{9,11},{10,... | collective-permute-start | bytes 344072 | tf_op jit(solution)/shard_map/ppermute | solution.py:46
  51.7 4.9 %collective-permute-start.10 = (bf16[16,3584]{1,0:T(8,128)(2,1)S(1)}, bf16[16,3584]{1,0:T(8,128)(2,1)S(1)}, u32[]{:S(2)}, u32[]{:S(2)}) collective-permute-start(bf16[16,3584]{1,0:T(8,128)(2,1)S(1)} %get-tuple-element.27), channel_id=1, source_target_pairs={{0,2},{1,3},{2,0},{3,1},{4,6},{5,7},{6,4},{7,5},{8,10},{9,11},{10,... | collective-permute-start | bytes 344072 | tf_op jit(solution)/shard_map/ppermute | solution.py:46
  55.3 1.6 %collective-permute-start.13 = (bf16[32,3584]{1,0:T(8,128)(2,1)S(1)}, bf16[32,3584]{1,0:T(8,128)(2,1)S(1)}, u32[]{:S(2)}, u32[]{:S(2)}) collective-permute-start(bf16[32,3584]{1,0:T(8,128)(2,1)S(1)} %pad_maximum_fusion.5), channel_id=1, source_target_pairs={{0,1},{1,0},{2,3},{3,2},{4,5},{5,4},{6,7},{7,6},{8,9},{9,8},{10,11... | collective-permute-start | bytes 688136 | tf_op jit(solution)/shard_map/ppermute | solution.py:46
  56.6 4.3 %collective-permute-start.11 = (bf16[32,3584]{1,0:T(8,128)(2,1)S(1)}, bf16[32,3584]{1,0:T(8,128)(2,1)S(1)}, u32[]{:S(2)}, u32[]{:S(2)}) collective-permute-start(bf16[32,3584]{1,0:T(8,128)(2,1)S(1)} %pad_maximum_fusion.4), channel_id=1, source_target_pairs={{0,1},{1,0},{2,3},{3,2},{4,5},{5,4},{6,7},{7,6},{8,9},{9,8},{10,11... | collective-permute-start | bytes 688136 | tf_op jit(solution)/shard_map/ppermute | solution.py:46
  65.1 6.9 %collective-permute-start.16 = (bf16[16,2048]{1,0:T(8,128)(2,1)S(1)}, bf16[16,2048]{1,0:T(8,128)(2,1)S(1)}, u32[]{:S(2)}, u32[]{:S(2)}) collective-permute-start(bf16[16,2048]{1,0:T(8,128)(2,1)S(1)} %get-tuple-element.43), channel_id=1, source_target_pairs={{0,12},{4,8},{8,4},{12,0},{1,13},{5,9},{9,5},{13,1},{2,14},{6,10},... | collective-permute-start | bytes 196616 | tf_op jit(solution)/shard_map/ppermute | solution.py:46
  67.6 6.5 %collective-permute-start.15 = (bf16[16,2048]{1,0:T(8,128)(2,1)S(1)}, bf16[16,2048]{1,0:T(8,128)(2,1)S(1)}, u32[]{:S(2)}, u32[]{:S(2)}) collective-permute-start(bf16[16,2048]{1,0:T(8,128)(2,1)S(1)} %get-tuple-element.44), channel_id=1, source_target_pairs={{0,8},{4,12},{8,0},{12,4},{1,9},{5,13},{9,1},{13,5},{2,10},{6,14},... | collective-permute-start | bytes 196616 | tf_op jit(solution)/shard_map/ppermute | solution.py:46
  67.6 6.5 %collective-permute-start.14 = (bf16[16,2048]{1,0:T(8,128)(2,1)S(1)}, bf16[16,2048]{1,0:T(8,128)(2,1)S(1)}, u32[]{:S(2)}, u32[]{:S(2)}) collective-permute-start(bf16[16,2048]{1,0:T(8,128)(2,1)S(1)} %get-tuple-element.42), channel_id=1, source_target_pairs={{0,4},{4,0},{8,12},{12,8},{1,5},{5,1},{9,13},{13,9},{2,6},{6,2},{1... | collective-permute-start | bytes 196616 | tf_op jit(solution)/shard_map/ppermute | solution.py:46
